TPU v7x, 1024 devices: a whole 8x8x8 slice. The times are simulated.
1024 devices in a mesh: band: 16 (over z, core), px: 16 (over y_lo, x), py: 4 (over y_hi).
Axes of the slice: x: 8, y: 8 (y_hi: 4, y_lo: 2; y = y_hi * 2 + y_lo), z: 8, core: 2. Of those that a mesh axis runs over, the one named last changes fastest.
Arguments:
- orbitals: bfloat16 [16, 8192, 384], P('band', ('px', 'py')), may hold values from -0.001953125 to 0.001953125
- occupations: float32 [16], P('band'), may hold values from 0.2 to 2
- stick_map: int32 [2, 8192], P(None, 'px'), may hold values from 0 to 191, as said below
- core_density: float32 [192, 192, 192], P('py', 'px'), may hold values from 0.05 to 0.5
Outputs:
- potential: float32 [192, 192, 192], P('py', 'px')
- gradient: float32 [3, 192, 192, 192], P(None, 'py', 'px')
Inputs may be any that keep to these rules, and one draw needn't show every extreme that they name: `stick_map`: columns i * 128 * 4 to (i + 1) * 128 * 4 - 1 have x index from i * 12 to (i + 1) * 12 - 1; no two columns share a grid position.
All inputs are finite; a program needn't handle non-finite values.
Results may differ from a plain program's by a relative error of at most 0.0054.
Values may be sent and summed in bfloat16 or wider, within the bound.
A program may use at most 64 MiB of HBM per device.

v0:
```python
import functools
import math

import jax
import jax.numpy as jnp
import numpy as np
from jax import lax
from jax.experimental import pallas as pl
from jax.experimental.pallas import tpu as pltpu
from jax.sharding import PartitionSpec as P

N = 192
SPACING = 0.25
KAPPA = 0.804
MU = 0.2195
SLATER = 0.75 * (3.0 / math.pi) ** (1.0 / 3.0)
REDUCED = 4.0 * (3.0 * math.pi**2) ** (2.0 / 3.0)
UNIT = 2.0 * math.pi / (N * SPACING)
F32 = jnp.float32
BF = jnp.bfloat16
MESH = pl.DeviceIdType.MESH
roll = pltpu.roll


def hilo(a):
    a = np.asarray(a, np.float32)
    hi = a.astype(BF)
    lo = (a - hi.astype(np.float32)).astype(BF)
    return np.stack([hi, lo])


def real_basis():
    n = np.arange(N)
    k = np.where(n <= 96, n, n - 96)
    cosine = n <= 96
    x = np.arange(N)
    angle = 2 * np.pi * (k[:, None] * x[None, :] % N) / N
    forward = np.where(cosine[:, None], np.cos(angle), np.sin(angle))
    weight = np.where((k == 0) | (k == 96), 1.0, 2.0)
    weight = np.where(cosine, weight, 2.0) / N
    inverse = (forward * weight[:, None]).T
    g = np.where(k == 96, 0.0, k) * UNIT
    slope = np.where(cosine[:, None], -np.sin(angle), np.cos(angle)) * (g * weight)[:, None]
    return forward, inverse, slope.T, (UNIT * k) ** 2


def make_tables():
    fwd, inv, dif, q2 = real_basis()
    idx = np.arange(N)
    ang = 2 * np.pi * (idx[:, None] * idx[None, :] % N) / N
    c, s = np.cos(ang), np.sin(ang)
    ta = np.zeros((64, 8, 384))
    for j in range(3):
        z = 3 * np.arange(64) + j
        ta[:, j, :N], ta[:, j, N:] = c[z], -s[z]
        ta[:, 3 + j, :N], ta[:, 3 + j, N:] = s[z], c[z]
    tyc = np.zeros((256, 512))
    tyc[:N, :N], tyc[:N, 256 : 256 + N] = c, s
    tx = np.zeros((384, 256))
    xp = 16 * (idx // 12) + idx % 12
    tx[:N, xp], tx[N:, xp] = c, s
    band = idx // 12
    krow = 128 * (band % 2) + 16 * (band // 2) + idx % 12
    ry = np.zeros((256, 256))
    ry[krow, :N] = fwd
    px, py, i = idx // 12, (idx % 12) // 3, idx % 3
    rx = np.zeros((N, 256))
    rx[:, 64 * i + 16 * py + px] = fwd.T
    rx[:, 192] = fwd[0]
    zo = (3 * np.arange(64)[None, :] + np.arange(3)[:, None]).reshape(-1)
    rz = fwd[:, zo]
    hz = inv[zo, :]
    gz = (dif @ fwd)[zo][:, zo]
    kcol = 16 * (idx % 12) + 8 * (band % 2) + band // 2
    ryi = np.zeros((2, 256, N))
    ryi[0][np.ix_(xp, kcol)] = inv
    ryi[1][np.ix_(xp, kcol)] = dif
    kx = 16 * (4 * i + py) + px
    rxi = np.zeros((256, 512))
    rxi[kx, :N] = inv.T
    rxi[kx, 256 : 256 + N] = dif.T
    qx = np.zeros((64, 1, 128), np.float32)
    qy = np.zeros((16, 1, 128), np.float32)
    for ii in range(3):
        for t in range(12):
            p = np.arange(64)
            qx[:, 0, 12 * ii + t] = q2[12 * (p % 16) + 3 * (p // 16) + ii]
            qy[:, 0, 12 * ii + t] = q2[12 * np.arange(16) + t]
    qz = np.broadcast_to(q2[:, None], (N, 128)).astype(np.float32)
    tabs = [hilo(a) for a in (ta.reshape(512, 384), tyc, tx, ry, rx, rz, hz, gz, ryi, rxi)]
    return tabs + [qx, qy, qz]


def mm(a, b):
    return lax.dot_general(a, b, (((1,), (0,)), ((), ())), preferred_element_type=F32)


def mmt(a, b):
    return lax.dot_general(a, b, (((1,), (1,)), ((), ())), preferred_element_type=F32)


def split(x):
    hi = x.astype(BF)
    return hi, (x - hi.astype(F32)).astype(BF)


def mm3(a, b, dot=mm):
    return dot(a[0], b[0]) + dot(a[0], b[1]) + dot(a[1], b[0])


def stage_columns(orb, x_of, y_of, px, ta):
    out = mmt(ta[0], orb) + mmt(ta[1], orb)
    row = lax.broadcasted_iota(jnp.int32, (8, 128), 0)
    place = jnp.where(row == 6, (x_of - px * 12).astype(F32), jnp.where(row == 7, y_of.astype(F32), 0.0))
    return (out.reshape(64, 8, 128) + place[None]).astype(BF)


def stage_scatter(pieces):
    data = jnp.concatenate(pieces, axis=1).astype(F32)
    hot = (lax.broadcasted_iota(jnp.int32, (256, 512), 0).astype(F32) == data[7:8]).astype(F32).astype(BF)
    place = lax.broadcasted_iota(jnp.int32, (16, 512), 0).astype(F32) == data[6:7]
    rows = jnp.concatenate([jnp.where(place, data[r : r + 1], 0.0) for r in range(6)], axis=0)
    return mmt(rows.astype(BF), hot).astype(BF)


def stage_density(p_re, p_im, weight, tyc, tx):
    a = mm(p_re, tyc[0]) + mm(p_re, tyc[1])
    b = mm(p_im, tyc[0]) + mm(p_im, tyc[1])
    y_re = (a[:, :256] - b[:, 256:]).astype(BF)
    y_im = (a[:, 256:] + b[:, :256]).astype(BF)
    a = mm(tx[0], y_re) + mm(tx[1], y_re)
    b = mm(tx[0], y_im) + mm(tx[1], y_im)
    re = a[:N] - b[N:]
    im = a[N:] + b[:N]
    return weight * (re * re + im * im)


def stage_plane(rho, ry, rx):
    t = mm3(ry, split(rho), mmt)
    return mm3(split(t), rx)


def stage_core(core, band, ry, rx):
    core = jnp.concatenate([core, jnp.zeros((4, N), F32)], axis=0)
    part = split(mm3(split(core), rx))
    y = lax.broadcasted_iota(jnp.int32, (256, 16), 0)
    t = lax.broadcasted_iota(jnp.int32, (256, 16), 1)
    pick = jnp.where((y == 12 * band + t) & (t < 12), 1.0, 0.0).astype(BF)
    placed = [mm(pick, h).astype(BF) for h in part]
    return mm3(ry, placed)


def halves_for_wire(x):
    lane = lax.broadcasted_iota(jnp.int32, x.shape, x.ndim - 1)
    return jnp.where(lane == 192, x - x.astype(BF).astype(F32), x).astype(BF)


def stage_pack(s):
    gap = jnp.zeros((24, 256), F32)
    rows = jnp.concatenate([s[0], gap, s[1], gap, s[2], gap, gap[:8]], axis=0)
    t = rows.T
    return t[0:64] + t[192:256] + roll(t[64:128], 12, 1) + roll(t[128:192], 24, 1)


def stage_z(w, qx, qy, qz, rz, hz, gz):
    lane = lax.broadcasted_iota(jnp.int32, (64, 128), 1)
    inside = lane < 36
    cols = jnp.concatenate([jnp.where(inside, w if j == 0 else roll(w, 128 - 40 * j, 1), 0.0) for j in range(3)], axis=0)
    both = split(cols)
    spectrum = mm3(rz, both)
    squared = qz + (qx + qy)
    factor = jnp.where(squared > 0, 4.0 * math.pi / jnp.where(squared > 0, squared, 1.0), 0.0)
    hart = mm3(hz, split(spectrum * factor))
    slope = mm3(gz, both)
    full = cols + roll(hart, 40, 1) + roll(slope, 80, 1)
    group = jnp.where(lane % 40 < 36, lane % 40 // 12, 9)
    out = []
    for i in range(3):
        acc = jnp.zeros((64, 128), F32)
        for j in range(3):
            shift = (12 * (j - i)) % 128
            part = full[64 * j : 64 * j + 64]
            acc = jnp.where(group == j, roll(part, shift, 1) if shift else part, acc)
        out.append(acc)
    return out


def swap_minor(x):
    lane = lax.broadcasted_iota(jnp.int32, (16, 128), 1)
    moved = [x[u] if u == 0 else roll(x[u], u, 1) for u in range(12)]
    out = []
    for v in range(12):
        at = lane - v
        at = jnp.where((at >= 0) & (at < 120) & (at % 40 < 36), at % 40 % 12, 99)
        acc = jnp.zeros((16, 128), F32)
        for u in range(12):
            acc = jnp.where(at == u, moved[u], acc)
        out.append(acc if v == 0 else roll(acc, 128 - v, 1))
    return out


def stage_y(x, ryi):
    cols = split(jnp.concatenate(swap_minor(x), axis=0))
    return mm3((ryi[0][0], ryi[1][0]), cols), mm3((ryi[0][1], ryi[1][1]), cols)


def stage_x(a, g, rxi):
    fill = jnp.zeros((64, 128), F32)
    f = jnp.concatenate(swap_minor(a) + [fill], axis=0).T.astype(BF)
    s = jnp.concatenate(swap_minor(g) + [fill], axis=0).T.astype(BF)
    both = mm(f, rxi[0]) + mm(f, rxi[1])
    gy = mm(s[0:64], rxi[0][:, :256]) + mm(s[0:64], rxi[1][:, :256])
    return both[0:40, :256], both[40:80, :256], both[0:40, 256:], gy[0:40], both[80:120, :256]


def stage_potential(rho, hart, gx, gy, gz):
    rho = jnp.where(rho > 0, rho, 1.0)
    cube_root = jnp.exp(jnp.log(rho) * (1.0 / 3.0))
    four = rho * cube_root
    reduced = (gx * gx + gy * gy + gz * gz) / (REDUCED * four * four)
    inverse = 1.0 / (1.0 + MU * reduced / KAPPA)
    enhance = 1.0 + KAPPA - KAPPA * inverse
    slope = MU * inverse * inverse
    return hart - SLATER * cube_root * ((4.0 / 3.0) * enhance - (8.0 / 3.0) * reduced * slope)


def stage_block(fields):
    lane = lax.broadcasted_iota(jnp.int32, (40, 128), 1)
    rows = [f[:, :128] for f in fields]
    for k in (0, 2):
        rows.append(jnp.where(lane < 64, fields[k][:, 128:], roll(fields[k + 1][:, 128:], 64, 1)))
    return jnp.concatenate(rows, axis=0).astype(BF)


def kernel(
    orb, occ, sticks, core, ta, tyc, tx, ry, rx, rz, hz, gz, ryi, rxi, qx, qy, qz,
    pot, grad,
    s1, r1a, r1b, core_in, planes, part, r2a, sums, r2b, s3, r3a, r3b, s4, r4a, r4b, r4c,
    s5, r5a, r5b, wide, r6, send, recv,
):
    band, px, py = lax.axis_index("band"), lax.axis_index("px"), lax.axis_index("py")
    cz, cc = band // 2, band % 2
    cx, lo = px % 8, px // 8
    cy = 2 * py + lo

    def at(z=None, c=None, x=None, y=None):
        z, c = cz if z is None else z, cc if c is None else c
        x, y = cx if x is None else x, cy if y is None else y
        return (z * 2 + c, (y % 2) * 8 + x, y // 2)

    def ring(me, d, n):
        return lax.rem(me + d, n)

    bar = pltpu.get_barrier_semaphore()

    def hail(target):
        pl.semaphore_signal(bar, inc=1, device_id=target, device_id_type=MESH)

    swapped = (px, band, py)
    for d in range(1, 8):
        hail(at(x=ring(cx, d, 8)))
        hail(at(y=ring(cy, d, 8)))
        hail(at(z=ring(cz, d, 8)))
    hail(at(c=1 - cc))

    @pl.when(band != px)
    def _():
        hail(swapped)

    count = [0]

    def copy(src, dst, target):
        k = count[0]
        count[0] += 1
        c = pltpu.make_async_remote_copy(
            src_ref=src, dst_ref=dst, send_sem=send.at[k], recv_sem=recv.at[k],
            device_id=target, device_id_type=MESH,
        )
        c.start()
        return c

    mine = pl.ds(pl.multiple_of(py * 128, 128), 128)
    s1[...] = stage_columns(orb[...], sticks[0:1, mine], sticks[1:2, mine], px, ta).reshape(8, 8, 8, 128)
    pl.semaphore_wait(bar, 22 + jnp.where(band != px, 1, 0))

    flights = [copy(s1.at[ring(cy, d, 8)], r1a.at[cy], at(y=ring(cy, d, 8))) for d in range(1, 8)]
    rows = core.at[pl.ds(3 * band, 3)]
    core_copy = pltpu.make_async_remote_copy(
        src_ref=rows, dst_ref=core_in, send_sem=send.at[80], recv_sem=recv.at[80],
        device_id=swapped, device_id_type=MESH,
    )
    own_copy = pltpu.make_async_copy(rows, core_in, send.at[81])

    @pl.when(band != px)
    def _():
        core_copy.start()

    @pl.when(band == px)
    def _():
        own_copy.start()

    r1a[cy] = s1[cy]
    for f in flights:
        f.wait()
    flights = [copy(r1a.at[:, ring(cx, d, 8)], r1b.at[:, cx], at(x=ring(cx, d, 8))) for d in range(1, 8)]
    for y in range(8):
        r1b[y, cx] = r1a[y, cx]

    @pl.when(band != px)
    def _():
        core_copy.wait()

    @pl.when(band == px)
    def _():
        own_copy.wait()

    def core_step(j, carry):
        part[j] = stage_core(core_in[j], band, ry, rx)
        return carry

    lax.fori_loop(0, 3, core_step, 0)
    for f in flights:
        f.wait()

    def scatter_step(k, carry):
        block = stage_scatter([r1b[2 * q + k // 8, k % 8] for q in range(4)])
        for r in range(6):
            planes[r, pl.ds(pl.multiple_of(k * 16, 16), 16), :] = block[16 * r : 16 * r + 16]
        return carry

    lax.fori_loop(0, 16, scatter_step, 0)

    def plane_step(j, carry):
        rho = stage_density(planes[j], planes[3 + j], occ[0, 0], tyc, tx)
        part[j] = part[j] + stage_plane(rho, ry, rx)
        return carry

    lax.fori_loop(0, 3, plane_step, 0)

    other = 1 - cc
    f = copy(part.at[:, pl.ds(pl.multiple_of(other * 128, 128), 128)], r2a, at(c=other))
    f.wait()
    for j in range(3):
        total = part[j, pl.ds(pl.multiple_of(cc * 128, 128), 128)] + r2a[j]
        sums[j] = halves_for_wire(total).reshape(8, 16, 256)
    flights = [copy(sums.at[:, ring(cz, d, 8)], r2b.at[cz], at(z=ring(cz, d, 8))) for d in range(1, 8)]
    r2b[cz] = sums[:, cz]
    for f in flights:
        f.wait()
    acc = r2b[0].astype(F32)
    for z in range(1, 8):
        acc = acc + r2b[z].astype(F32)

    s3[...] = stage_pack(acc).reshape(8, 8, 128)
    flights = [copy(s3.at[ring(cy, d, 8)], r3a.at[cy], at(y=ring(cy, d, 8))) for d in range(1, 8)]
    r3a[cy] = s3[cy]
    for f in flights:
        f.wait()
    flights = [
        copy(r3a.at[:, pl.ds(ring(cx, d, 8), 1)], r3b.at[:, pl.ds(cx, 1)], at(x=ring(cx, d, 8))) for d in range(1, 8)
    ]
    r3b[:, pl.ds(cx, 1)] = r3a[:, pl.ds(cx, 1)]
    for f in flights:
        f.wait()
    out = stage_z(r3b[...].reshape(64, 128), qx[py * 16 + px], qy[band], qz[...], rz, hz, gz)

    for i in range(3):
        s4[:, i] = out[i].reshape(4, 16, 128)
    flights = [
        copy(s4.at[ring(py, d, 4)], r4a.at[py], at(y=2 * ring(py, d, 4) + lo)) for d in range(1, 4)
    ]
    r4a[py] = s4[py]
    for f in flights:
        f.wait()
    f = copy(r4a.at[:, :, pl.ds(pl.multiple_of(other * 8, 8), 8)], r4b.at[cc], at(c=other))
    r4b[cc] = r4a[:, :, pl.ds(pl.multiple_of(cc * 8, 8), 8)]
    f.wait()
    flights = [
        copy(r4b.at[:, :, :, pl.ds(ring(cz, d, 8), 1)], r4c.at[:, :, :, pl.ds(cz, 1)], at(z=ring(cz, d, 8)))
        for d in range(1, 8)
    ]
    r4c[:, :, :, pl.ds(cz, 1)] = r4b[:, :, :, pl.ds(cz, 1)]
    for f in flights:
        f.wait()
    x = [jnp.concatenate([r4c[0, q, i], r4c[1, q, i]], axis=0) for i in range(3) for q in range(4)]
    along, slope = stage_y(x, ryi)

    s5[:, :, 0] = along.astype(BF).reshape(2, 8, 16, 128)
    s5[:, :, 1] = slope.astype(BF).reshape(2, 8, 16, 128)
    f = copy(s5.at[1 - lo], r5a.at[lo], at(y=2 * py + 1 - lo))
    r5a[lo] = s5[lo]
    f.wait()
    flights = [copy(r5a.at[:, ring(cx, d, 8)], r5b.at[:, cx], at(x=ring(cx, d, 8))) for d in range(1, 8)]
    for q in range(2):
        r5b[q, cx] = r5a[q, cx]
    for f in flights:
        f.wait()
    wide[...] = r5b[...].astype(F32).reshape(512, 128)
    a = [wide[pl.ds(y, 16, stride=32), :] for y in range(12)]
    g = [wide[pl.ds(16 + y, 16, stride=32), :] for y in range(12)]
    rho, hart, gx, gy, gzz = stage_x(a, g, rxi)
    value = stage_potential(rho, hart, gx, gy, gzz)

    r6[cc, cz] = stage_block([value, gx, gy, gzz])
    flights = [copy(r6.at[cc, cz], r6.at[cc, cz], at(z=ring(cz, d, 8))) for d in range(1, 8)]
    last = [copy(r6.at[cc, cz], r6.at[cc, cz], at(c=other))]
    for d in range(1, 8):
        flights[d - 1].wait_recv()
        z = ring(cz, 8 - d, 8)
        last.append(copy(r6.at[cc, z], r6.at[cc, z], at(c=other)))
    for f in flights:
        f.wait_send()
    for f in last:
        f.wait()

    def lay(s, carry):
        v = r6[s // 8, s % 8].astype(F32)
        tail = roll(v, 64, 1)
        for k in range(4):
            half = (v, tail)[k % 2]
            for j in range(3):
                r, h = 40 * k + 12 * j, 160 + 40 * (k // 2) + 12 * j
                ref = pot.at[3 * s + j] if k == 0 else grad.at[k - 1, 3 * s + j]
                ref[:, 0:128] = v[r : r + 12]
                ref[:, 128:192] = half[h : h + 12, 0:64]
        return carry

    lax.fori_loop(0, 16, lay, 0)


def body(orbitals, occupations, stick_map, core_density):
    tables = make_tables()
    vmem = pl.BlockSpec(memory_space=pltpu.VMEM)
    scratch = [
        pltpu.VMEM((8, 8, 8, 128), BF),
        pltpu.VMEM((8, 8, 8, 128), BF),
        pltpu.VMEM((8, 8, 8, 128), BF),
        pltpu.VMEM((3, 12, N), F32),
        pltpu.VMEM((6, 256, 256), BF),
        pltpu.VMEM((3, 256, 256), F32),
        pltpu.VMEM((3, 128, 256), F32),
        pltpu.VMEM((3, 8, 16, 256), BF),
        pltpu.VMEM((8, 3, 16, 256), BF),
        pltpu.VMEM((8, 8, 128), F32),
        pltpu.VMEM((8, 8, 128), F32),
        pltpu.VMEM((8, 8, 128), F32),
        pltpu.VMEM((4, 3, 16, 128), F32),
        pltpu.VMEM((4, 3, 16, 128), F32),
        pltpu.VMEM((2, 4, 3, 8, 128), F32),
        pltpu.VMEM((2, 4, 3, 8, 128), F32),
        pltpu.VMEM((2, 8, 2, 16, 128), BF),
        pltpu.VMEM((2, 8, 2, 16, 128), BF),
        pltpu.VMEM((2, 8, 2, 16, 128), BF),
        pltpu.VMEM((512, 128), F32),
        pltpu.VMEM((2, 8, 240, 128), BF),
        pltpu.SemaphoreType.DMA((82,)),
        pltpu.SemaphoreType.DMA((82,)),
    ]
    return pl.pallas_call(
        kernel,
        out_shape=(
            jax.ShapeDtypeStruct((48, 12, N), F32),
            jax.ShapeDtypeStruct((3, 48, 12, N), F32),
        ),
        in_specs=[vmem, pl.BlockSpec(memory_space=pltpu.SMEM), vmem, pl.BlockSpec(memory_space=pl.ANY)]
        + [vmem] * len(tables),
        out_specs=(vmem, vmem),
        scratch_shapes=scratch,
        compiler_params=pltpu.CompilerParams(collective_id=0, has_side_effects=True, vmem_limit_bytes=60 * 1024 * 1024),
    )(orbitals[0], occupations.reshape(1, 1), stick_map, core_density, *tables)


def solution(mesh):
    return jax.shard_map(
        body,
        mesh=mesh,
        in_specs=(P("band", ("px", "py"), None), P("band"), P(None, "px"), P("py", "px", None)),
        out_specs=(P("py", "px", None), P(None, "py", "px", None)),
        check_vma=False,
    )
```

profile of v0, /device:TPU:1, one launch (start us, length us, event | category | flops | bytes accessed | tf_op | source)
XLA Modules:
  0.0 115.4 jit_solution(11828692324131036313)
XLA Ops:
  1.3 2.3 %copy.19.core = f32[48,12,192]{2,1,0:T(8,128)} copy(f32[48,12,192]{2,0,1:T(8,128)} %param.20) | data formatting | bytes 884736 | tf_op args[3]
  3.6 105.6 %shard_map.176 = (f32[48,12,192]{2,1,0:T(8,128)}, f32[3,48,12,192]{3,2,1,0:T(8,128)}) custom-call(bf16[128,384]{1,0:T(8,128)(2,1)} %bitcast.3, f32[1,1]{1,0:T(1,128)} %bitcast.2.occ, s32[2,512]{1,0:T(2,128)} %sticks.1, f32[48,12,192]{2,1,0:T(8,128)} %copy.19.core, bf16[2,512,384]{2,1,0:T(8,128)(2,1)} %constant.26.clone.ta, ...), custom_call_target="tpu_custom_call" | custom-call | tf_op jit(solution)/shard_map/pallas_call | solution.py:459
  109.2 2.3 %copy.20 = f32[48,12,192]{2,0,1:T(8,128)} copy(f32[48,12,192]{2,1,0:T(8,128)} %get-tuple-element.2) | data formatting | bytes 884736 | tf_op jit(solution)/shard_map/pallas_call | solution.py:459
  111.5 3.9 %copy.21 = f32[3,48,12,192]{3,1,2,0:T(8,128)} copy(f32[3,48,12,192]{3,2,1,0:T(8,128)} %get-tuple-element.3) | data formatting | bytes 2654208 | tf_op jit(solution)/shard_map/pallas_call | solution.py:459
where the time goes:
time: 116 us; the launch traced here: 115 us
  Pallas kernels  106 us (91%)
  local copies, waits for them, and re-layouts  8.49 us (7%)
  between operations  1.29 us (1%)
    pallas_call x1, Pallas kernels, body(): pl.pallas_call(kernel, out_shape=(jax.ShapeDtypeStruct((48, 12, N), F32),...  106 us
    pallas_call x2, local copies, waits for them, and re-layouts, body(): pl.pallas_call(kernel, out_shape=(jax.ShapeDtypeStruct((48, 12, N), F32),...  6.19 us

commit v1 on v0

--- a/solution.py
+++ b/solution.py
@@ -54,11 +54,9 @@
         z = 3 * np.arange(64) + j
         ta[:, j, :N], ta[:, j, N:] = c[z], -s[z]
         ta[:, 3 + j, :N], ta[:, 3 + j, N:] = s[z], c[z]
+    xp = 16 * (idx // 12) + idx % 12
     tyc = np.zeros((256, 512))
-    tyc[:N, :N], tyc[:N, 256 : 256 + N] = c, s
-    tx = np.zeros((384, 256))
-    xp = 16 * (idx // 12) + idx % 12
-    tx[:N, xp], tx[N:, xp] = c, s
+    tyc[xp, :N], tyc[xp, 256 : 256 + N] = c, s
     band = idx // 12
     krow = 128 * (band % 2) + 16 * (band // 2) + idx % 12
     ry = np.zeros((256, 256))
@@ -69,14 +67,13 @@
     rx[:, 192] = fwd[0]
     zo = (3 * np.arange(64)[None, :] + np.arange(3)[:, None]).reshape(-1)
     rz = fwd[:, zo]
-    hz = inv[zo, :]
     gz = (dif @ fwd)[zo][:, zo]
     kcol = 16 * (idx % 12) + 8 * (band % 2) + band // 2
     ryi = np.zeros((2, 256, N))
     ryi[0][np.ix_(xp, kcol)] = inv
     ryi[1][np.ix_(xp, kcol)] = dif
     kx = 16 * (4 * i + py) + px
-    rxi = np.zeros((256, 512))
+    rxi = np.zeros((N, 512))
     rxi[kx, :N] = inv.T
     rxi[kx, 256 : 256 + N] = dif.T
     qx = np.zeros((64, 1, 128), np.float32)
@@ -86,9 +83,8 @@
             p = np.arange(64)
             qx[:, 0, 12 * ii + t] = q2[12 * (p % 16) + 3 * (p // 16) + ii]
             qy[:, 0, 12 * ii + t] = q2[12 * np.arange(16) + t]
-    qz = np.broadcast_to(q2[:, None], (N, 128)).astype(np.float32)
-    tabs = [hilo(a) for a in (ta.reshape(512, 384), tyc, tx, ry, rx, rz, hz, gz, ryi, rxi)]
-    return tabs + [qx, qy, qz]
+    tabs = [hilo(a) for a in (ta.reshape(512, 384), tyc, ry, rx, rz, gz, ryi, rxi)]
+    return tabs + [qx, qy]
 
 
 def mm(a, b):
@@ -104,6 +100,10 @@
     return hi, (x - hi.astype(F32)).astype(BF)
 
 
+def mtm(a, b):
+    return lax.dot_general(a, b, (((0,), (0,)), ((), ())), preferred_element_type=F32)
+
+
 def mm3(a, b, dot=mm):
     return dot(a[0], b[0]) + dot(a[0], b[1]) + dot(a[1], b[0])
 
@@ -111,7 +111,8 @@
 def stage_columns(orb, x_of, y_of, px, ta):
     out = mmt(ta[0], orb) + mmt(ta[1], orb)
     row = lax.broadcasted_iota(jnp.int32, (8, 128), 0)
-    place = jnp.where(row == 6, (x_of - px * 12).astype(F32), jnp.where(row == 7, y_of.astype(F32), 0.0))
+    y_row = y_of + 4 * (y_of // 12)
+    place = jnp.where(row == 6, (x_of - px * 12).astype(F32), jnp.where(row == 7, y_row.astype(F32), 0.0))
     return (out.reshape(64, 8, 128) + place[None]).astype(BF)
 
 
@@ -130,8 +131,8 @@
     y_im = (a[:, 256:] + b[:, :256]).astype(BF)
     a = mm(tx[0], y_re) + mm(tx[1], y_re)
     b = mm(tx[0], y_im) + mm(tx[1], y_im)
-    re = a[:N] - b[N:]
-    im = a[N:] + b[:N]
+    re = a[:N] - b[256 : 256 + N]
+    im = a[256 : 256 + N] + b[:N]
     return weight * (re * re + im * im)
 
 
@@ -162,15 +163,18 @@
     return t[0:64] + t[192:256] + roll(t[64:128], 12, 1) + roll(t[128:192], 24, 1)
 
 
-def stage_z(w, qx, qy, qz, rz, hz, gz):
+def stage_z(w, qx, qy, rz, gz):
     lane = lax.broadcasted_iota(jnp.int32, (64, 128), 1)
     inside = lane < 36
     cols = jnp.concatenate([jnp.where(inside, w if j == 0 else roll(w, 128 - 40 * j, 1), 0.0) for j in range(3)], axis=0)
     both = split(cols)
     spectrum = mm3(rz, both)
-    squared = qz + (qx + qy)
+    n = lax.broadcasted_iota(jnp.int32, (N, 128), 0)
+    k = jnp.where(n <= 96, n, n - 96)
+    weight = jnp.where((n == 0) | (n == 96), 1.0 / N, 2.0 / N)
+    squared = UNIT**2 * (k * k).astype(F32) + (qx + qy)
     factor = jnp.where(squared > 0, 4.0 * math.pi / jnp.where(squared > 0, squared, 1.0), 0.0)
-    hart = mm3(hz, split(spectrum * factor))
+    hart = mm3(rz, split(spectrum * (factor * weight)), mtm)
     slope = mm3(gz, both)
     full = cols + roll(hart, 40, 1) + roll(slope, 80, 1)
     group = jnp.where(lane % 40 < 36, lane % 40 // 12, 9)
@@ -206,8 +210,8 @@
 
 def stage_x(a, g, rxi):
     fill = jnp.zeros((64, 128), F32)
-    f = jnp.concatenate(swap_minor(a) + [fill], axis=0).T.astype(BF)
-    s = jnp.concatenate(swap_minor(g) + [fill], axis=0).T.astype(BF)
+    f = jnp.concatenate(swap_minor(a) + [fill], axis=0).T[:, :N].astype(BF)
+    s = jnp.concatenate(swap_minor(g) + [fill], axis=0).T[:, :N].astype(BF)
     both = mm(f, rxi[0]) + mm(f, rxi[1])
     gy = mm(s[0:64], rxi[0][:, :256]) + mm(s[0:64], rxi[1][:, :256])
     return both[0:40, :256], both[40:80, :256], both[0:40, 256:], gy[0:40], both[80:120, :256]
@@ -233,10 +237,10 @@
 
 
 def kernel(
-    orb, occ, sticks, core, ta, tyc, tx, ry, rx, rz, hz, gz, ryi, rxi, qx, qy, qz,
-    pot, grad,
-    s1, r1a, r1b, core_in, planes, part, r2a, sums, r2b, s3, r3a, r3b, s4, r4a, r4b, r4c,
-    s5, r5a, r5b, wide, r6, send, recv,
+    orb, occ, sticks, core, ta, tyc, ry, rx, rz, gz, ryi, rxi, qx, qy,
+    r6,
+    tx, s1, r1a, r1b, core_out, core_in, planes, part, r2a, sums, r2b, s3, r3a, r3b, s4, r4a, r4b, r4c,
+    s5, r5a, r5b, wide, send, recv,
 ):
     band, px, py = lax.axis_index("band"), lax.axis_index("px"), lax.axis_index("py")
     cz, cc = band // 2, band % 2
@@ -247,6 +251,15 @@
         z, c = cz if z is None else z, cc if c is None else c
         x, y = cx if x is None else x, cy if y is None else y
         return (z * 2 + c, (y % 2) * 8 + x, y // 2)
+
+    open_scope = [None]
+
+    def phase(name):
+        if open_scope[0] is not None:
+            open_scope[0].__exit__(None, None, None)
+        open_scope[0] = jax.named_scope(name) if name else None
+        if name:
+            open_scope[0].__enter__()
 
     def ring(me, d, n):
         return lax.rem(me + d, n)
@@ -279,17 +292,22 @@
         c.start()
         return c
 
+    phase("columns")
     mine = pl.ds(pl.multiple_of(py * 128, 128), 128)
     s1[...] = stage_columns(orb[...], sticks[0:1, mine], sticks[1:2, mine], px, ta).reshape(8, 8, 8, 128)
+    for j in range(3):
+        core_out[j] = core[:, pl.ds(3 * band + j, 1)].reshape(12, N)
+    for h in range(2):
+        tx[h] = tyc[h].astype(F32).T.astype(BF)
+    phase("barrier")
     pl.semaphore_wait(bar, 22 + jnp.where(band != px, 1, 0))
 
+    phase("e1_y")
     flights = [copy(s1.at[ring(cy, d, 8)], r1a.at[cy], at(y=ring(cy, d, 8))) for d in range(1, 8)]
-    rows = core.at[pl.ds(3 * band, 3)]
     core_copy = pltpu.make_async_remote_copy(
-        src_ref=rows, dst_ref=core_in, send_sem=send.at[80], recv_sem=recv.at[80],
+        src_ref=core_out, dst_ref=core_in, send_sem=send.at[80], recv_sem=recv.at[80],
         device_id=swapped, device_id_type=MESH,
     )
-    own_copy = pltpu.make_async_copy(rows, core_in, send.at[81])
 
     @pl.when(band != px)
     def _():
@@ -297,11 +315,12 @@
 
     @pl.when(band == px)
     def _():
-        own_copy.start()
+        core_in[...] = core_out[...]
 
     r1a[cy] = s1[cy]
     for f in flights:
         f.wait()
+    phase("e1_x_core")
     flights = [copy(r1a.at[:, ring(cx, d, 8)], r1b.at[:, cx], at(x=ring(cx, d, 8))) for d in range(1, 8)]
     for y in range(8):
         r1b[y, cx] = r1a[y, cx]
@@ -310,18 +329,16 @@
     def _():
         core_copy.wait()
 
-    @pl.when(band == px)
-    def _():
-        own_copy.wait()
-
     def core_step(j, carry):
         part[j] = stage_core(core_in[j], band, ry, rx)
         return carry
 
     lax.fori_loop(0, 3, core_step, 0)
-    for f in flights:
-        f.wait()
-
+    phase("e1_x_wait")
+    for f in flights:
+        f.wait()
+
+    phase("scatter")
     def scatter_step(k, carry):
         block = stage_scatter([r1b[2 * q + k // 8, k % 8] for q in range(4)])
         for r in range(6):
@@ -330,6 +347,8 @@
 
     lax.fori_loop(0, 16, scatter_step, 0)
 
+    phase("plane")
+
     def plane_step(j, carry):
         rho = stage_density(planes[j], planes[3 + j], occ[0, 0], tyc, tx)
         part[j] = part[j] + stage_plane(rho, ry, rx)
@@ -337,12 +356,14 @@
 
     lax.fori_loop(0, 3, plane_step, 0)
 
+    phase("e2_core")
     other = 1 - cc
     f = copy(part.at[:, pl.ds(pl.multiple_of(other * 128, 128), 128)], r2a, at(c=other))
     f.wait()
     for j in range(3):
         total = part[j, pl.ds(pl.multiple_of(cc * 128, 128), 128)] + r2a[j]
         sums[j] = halves_for_wire(total).reshape(8, 16, 256)
+    phase("e2_z")
     flights = [copy(sums.at[:, ring(cz, d, 8)], r2b.at[cz], at(z=ring(cz, d, 8))) for d in range(1, 8)]
     r2b[cz] = sums[:, cz]
     for f in flights:
@@ -351,30 +372,37 @@
     for z in range(1, 8):
         acc = acc + r2b[z].astype(F32)
 
+    phase("pack")
     s3[...] = stage_pack(acc).reshape(8, 8, 128)
+    phase("e3_y")
     flights = [copy(s3.at[ring(cy, d, 8)], r3a.at[cy], at(y=ring(cy, d, 8))) for d in range(1, 8)]
     r3a[cy] = s3[cy]
     for f in flights:
         f.wait()
+    phase("e3_x")
     flights = [
         copy(r3a.at[:, pl.ds(ring(cx, d, 8), 1)], r3b.at[:, pl.ds(cx, 1)], at(x=ring(cx, d, 8))) for d in range(1, 8)
     ]
     r3b[:, pl.ds(cx, 1)] = r3a[:, pl.ds(cx, 1)]
     for f in flights:
         f.wait()
-    out = stage_z(r3b[...].reshape(64, 128), qx[py * 16 + px], qy[band], qz[...], rz, hz, gz)
+    phase("z")
+    out = stage_z(r3b[...].reshape(64, 128), qx[py * 16 + px], qy[band], rz, gz)
 
     for i in range(3):
         s4[:, i] = out[i].reshape(4, 16, 128)
+    phase("e4_y")
     flights = [
         copy(s4.at[ring(py, d, 4)], r4a.at[py], at(y=2 * ring(py, d, 4) + lo)) for d in range(1, 4)
     ]
     r4a[py] = s4[py]
     for f in flights:
         f.wait()
+    phase("e4_core")
     f = copy(r4a.at[:, :, pl.ds(pl.multiple_of(other * 8, 8), 8)], r4b.at[cc], at(c=other))
     r4b[cc] = r4a[:, :, pl.ds(pl.multiple_of(cc * 8, 8), 8)]
     f.wait()
+    phase("e4_z")
     flights = [
         copy(r4b.at[:, :, :, pl.ds(ring(cz, d, 8), 1)], r4c.at[:, :, :, pl.ds(cz, 1)], at(z=ring(cz, d, 8)))
         for d in range(1, 8)
@@ -382,19 +410,23 @@
     r4c[:, :, :, pl.ds(cz, 1)] = r4b[:, :, :, pl.ds(cz, 1)]
     for f in flights:
         f.wait()
+    phase("y")
     x = [jnp.concatenate([r4c[0, q, i], r4c[1, q, i]], axis=0) for i in range(3) for q in range(4)]
     along, slope = stage_y(x, ryi)
 
     s5[:, :, 0] = along.astype(BF).reshape(2, 8, 16, 128)
     s5[:, :, 1] = slope.astype(BF).reshape(2, 8, 16, 128)
+    phase("e5_y")
     f = copy(s5.at[1 - lo], r5a.at[lo], at(y=2 * py + 1 - lo))
     r5a[lo] = s5[lo]
     f.wait()
+    phase("e5_x")
     flights = [copy(r5a.at[:, ring(cx, d, 8)], r5b.at[:, cx], at(x=ring(cx, d, 8))) for d in range(1, 8)]
     for q in range(2):
         r5b[q, cx] = r5a[q, cx]
     for f in flights:
         f.wait()
+    phase("x")
     wide[...] = r5b[...].astype(F32).reshape(512, 128)
     a = [wide[pl.ds(y, 16, stride=32), :] for y in range(12)]
     g = [wide[pl.ds(16 + y, 16, stride=32), :] for y in range(12)]
@@ -402,6 +434,7 @@
     value = stage_potential(rho, hart, gx, gy, gzz)
 
     r6[cc, cz] = stage_block([value, gx, gy, gzz])
+    phase("e6")
     flights = [copy(r6.at[cc, cz], r6.at[cc, cz], at(z=ring(cz, d, 8))) for d in range(1, 8)]
     last = [copy(r6.at[cc, cz], r6.at[cc, cz], at(c=other))]
     for d in range(1, 8):
@@ -412,29 +445,36 @@
         f.wait_send()
     for f in last:
         f.wait()
-
-    def lay(s, carry):
-        v = r6[s // 8, s % 8].astype(F32)
-        tail = roll(v, 64, 1)
+    phase(None)
+
+
+def lay_kernel(r6, pot, grad, wide, woven):
+    wide[...] = r6[...].astype(F32).reshape(3840, 128)
+
+    def step(y, carry):
         for k in range(4):
-            half = (v, tail)[k % 2]
+            ref = pot.at[y] if k == 0 else grad.at[k - 1, y]
             for j in range(3):
-                r, h = 40 * k + 12 * j, 160 + 40 * (k // 2) + 12 * j
-                ref = pot.at[3 * s + j] if k == 0 else grad.at[k - 1, 3 * s + j]
-                ref[:, 0:128] = v[r : r + 12]
-                ref[:, 128:192] = half[h : h + 12, 0:64]
+                z = pl.ds(j, 16, stride=3)
+                woven[k, 0, z] = wide[pl.ds(40 * k + 12 * j + y, 16, stride=240), :]
+                tail = wide[pl.ds(160 + 40 * (k // 2) + 12 * j + y, 16, stride=240), :]
+                woven[k, 1, z] = roll(tail, 64, 1) if k % 2 else tail
+            ref[:, 0:128] = woven[k, 0]
+            ref[:, 128:192] = woven[k, 1, :, 0:64]
         return carry
 
-    lax.fori_loop(0, 16, lay, 0)
+    lax.fori_loop(0, 12, step, 0)
 
 
 def body(orbitals, occupations, stick_map, core_density):
     tables = make_tables()
     vmem = pl.BlockSpec(memory_space=pltpu.VMEM)
     scratch = [
+        pltpu.VMEM((2, 512, 256), BF),
         pltpu.VMEM((8, 8, 8, 128), BF),
         pltpu.VMEM((8, 8, 8, 128), BF),
         pltpu.VMEM((8, 8, 8, 128), BF),
+        pltpu.VMEM((3, 12, N), F32),
         pltpu.VMEM((3, 12, N), F32),
         pltpu.VMEM((6, 256, 256), BF),
         pltpu.VMEM((3, 256, 256), F32),
@@ -452,22 +492,30 @@
         pltpu.VMEM((2, 8, 2, 16, 128), BF),
         pltpu.VMEM((2, 8, 2, 16, 128), BF),
         pltpu.VMEM((512, 128), F32),
-        pltpu.VMEM((2, 8, 240, 128), BF),
         pltpu.SemaphoreType.DMA((82,)),
         pltpu.SemaphoreType.DMA((82,)),
     ]
-    return pl.pallas_call(
+    blocks = pl.pallas_call(
         kernel,
+        out_shape=jax.ShapeDtypeStruct((2, 8, 240, 128), BF),
+        in_specs=[vmem, pl.BlockSpec(memory_space=pltpu.SMEM), vmem, vmem]
+        + [vmem] * len(tables),
+        out_specs=vmem,
+        scratch_shapes=scratch,
+        compiler_params=pltpu.CompilerParams(collective_id=0, has_side_effects=True, vmem_limit_bytes=40 * 1024 * 1024),
+    )(orbitals[0], occupations.reshape(1, 1), stick_map, core_density.transpose(1, 0, 2), *tables)
+    pot, grad = pl.pallas_call(
+        lay_kernel,
         out_shape=(
-            jax.ShapeDtypeStruct((48, 12, N), F32),
-            jax.ShapeDtypeStruct((3, 48, 12, N), F32),
+            jax.ShapeDtypeStruct((12, 48, N), F32),
+            jax.ShapeDtypeStruct((3, 12, 48, N), F32),
         ),
-        in_specs=[vmem, pl.BlockSpec(memory_space=pltpu.SMEM), vmem, pl.BlockSpec(memory_space=pl.ANY)]
-        + [vmem] * len(tables),
+        in_specs=[vmem],
         out_specs=(vmem, vmem),
-        scratch_shapes=scratch,
-        compiler_params=pltpu.CompilerParams(collective_id=0, has_side_effects=True, vmem_limit_bytes=60 * 1024 * 1024),
-    )(orbitals[0], occupations.reshape(1, 1), stick_map, core_density, *tables)
+        scratch_shapes=[pltpu.VMEM((3840, 128), F32), pltpu.VMEM((4, 2, 48, 128), F32)],
+        compiler_params=pltpu.CompilerParams(vmem_limit_bytes=20 * 1024 * 1024),
+    )(blocks)
+    return pot.transpose(1, 0, 2), grad.transpose(0, 2, 1, 3)
 
 
 def solution(mesh):

time: 116 us -> 118 us (1.017)
  local copies, waits for them, and re-layouts: 8.49 us -> 12 us
  Pallas kernels: 106 us -> 104 us
    unnamed x1 -> x26, local copies, waits for them, and re-layouts: 2.3 us -> 12 us
    pallas_call x2 -> x0, local copies, waits for them, and re-layouts: 6.19 us -> none  [body(): pl.pallas_call(kernel, out_shape=(jax.ShapeDtypeStruct((48, 12, N), F32),...]
    pallas_call x1 -> x2, Pallas kernels: 106 us -> 104 us  [the longest x1 101 us: body(): pl.pallas_call(kernel, out_shape=jax.ShapeDtypeStruct((2, 8, 240, 128), B...]
where the time goes in v1:
time: 118 us; the launch traced here: 117 us
  Pallas kernels  104 us (88%)
  local copies, waits for them, and re-layouts  12 us (10%)
  between operations  1.3 us (1%)
    pallas_call x1, Pallas kernels, body(): pl.pallas_call(kernel, out_shape=jax.ShapeDtypeStruct((2, 8, 240, 128), B...  101 us
    unnamed x26, local copies, waits for them, and re-layouts  12 us
    pallas_call x1, Pallas kernels, body(): pl.pallas_call(lay_kernel, out_shape=(jax.ShapeDtypeStruct((12, 48, N), F...  2.67 us

profile of v1, /device:TPU:1, one launch (start us, length us, event | category | flops | bytes accessed | tf_op | source)
XLA Modules:
  0.0 117.1 jit_solution(6569270024959589649)
XLA Ops:
  1.3 0.0 copy-start
  1.3 1.1 copy-done
  2.4 0.0 copy-start.1
  2.4 1.1 copy-done.1
  3.5 0.0 copy-start.2
  3.5 1.0 copy-done.2
  4.5 0.0 copy-start.3
  4.5 1.0 copy-done.3
  5.6 1.0 copy-done.4
  6.6 0.0 copy-start.5
  6.6 0.9 copy-done.5
  7.5 0.0 copy-start.6
  7.5 0.9 copy-done.6
  8.4 0.0 copy-start.7
  8.4 0.9 copy-done.7
  9.4 0.0 copy-start.8
  9.4 0.9 copy-done.8
  10.3 0.0 copy-start.9
  10.3 0.9 copy-done.9
  11.2 0.8 copy-done.10
  11.9 0.7 copy-done.11
  12.6 0.7 copy-done.12
  13.3 101.1 %shard_map.149.r6 = bf16[2,8,240,128]{3,2,1,0:T(8,128)(2,1)S(1)} custom-call(bf16[128,384]{1,0:T(8,128)(2,1)S(1)} %bitcast.7, f32[1,1]{1,0:T(1,128)} %bitcast.5.occ, s32[2,512]{1,0:T(2,128)S(1)} %copy-done.12, f32[12,48,192]{2,1,0:T(8,128)S(1)} %bitcast.6, bf16[2,512,384]{2,1,0:T(8,128)(2,1)S(1)} %copy-done, bf16[2,256,512]{2,1,0:T(8,128)(2,1)S(1)} %copy-done.3, ...), custom_call_target="tpu_custom_call" | custom-call | tf_op jit(solution)/shard_map/pallas_call | solution.py:498
  114.4 2.7 %shard_map.150 = (f32[12,48,192]{2,1,0:T(8,128)}, f32[3,12,48,192]{3,2,1,0:T(8,128)}) custom-call(bf16[2,8,240,128]{3,2,1,0:T(8,128)(2,1)S(1)} %shard_map.149.r6), custom_call_target="tpu_custom_call" | custom-call | tf_op jit(solution)/shard_map/pallas_call | solution.py:507
  (4 shorter events, 0.0 us)
Async XLA Ops:
  1.3 1.1 copy-start
  2.4 1.1 copy-start.1
  3.5 1.0 copy-start.2
  4.5 1.0 copy-start.3
  5.6 1.0 copy-start.4
  6.6 0.9 copy-start.5
  7.5 0.9 copy-start.6
  8.4 0.9 copy-start.7
  9.4 0.9 copy-start.8
  10.3 0.9 copy-start.9
  11.2 0.8 copy-start.10
  11.9 0.7 copy-start.11
  12.6 0.7 copy-start.12

commit v2 on v1

--- a/solution.py
+++ b/solution.py
@@ -237,11 +237,15 @@
 
 
 def kernel(
-    orb, occ, sticks, core, ta, tyc, ry, rx, rz, gz, ryi, rxi, qx, qy,
-    r6,
-    tx, s1, r1a, r1b, core_out, core_in, planes, part, r2a, sums, r2b, s3, r3a, r3b, s4, r4a, r4b, r4c,
-    s5, r5a, r5b, wide, send, recv,
+    occ, *rest,
 ):
+    far, rest = rest[:13], rest[13:]
+    r6, near, rest = rest[0], rest[1:14], rest[14:]
+    orb, sticks, core, ta, tyc, ry, rx, rz, gz, ryi, rxi, qx, qy = near
+    (
+    tx, s1, r1a, r1b, core_out, core_in, planes, part, r2a, sums, r2b, s3, r3a, r3b, s4, r4a, r4c,
+    s5, r5b, wide, send, recv, load,
+    ) = rest
     band, px, py = lax.axis_index("band"), lax.axis_index("px"), lax.axis_index("py")
     cz, cc = band // 2, band % 2
     cx, lo = px % 8, px // 8
@@ -274,12 +278,18 @@
         hail(at(x=ring(cx, d, 8)))
         hail(at(y=ring(cy, d, 8)))
         hail(at(z=ring(cz, d, 8)))
+        hail(at(z=ring(cz, d, 8), c=1 - cc))
+        hail(at(x=ring(cx, d, 8), y=2 * py + 1 - lo))
     hail(at(c=1 - cc))
 
     @pl.when(band != px)
     def _():
         hail(swapped)
 
+    loads = {}
+    for k in (0, 1, 3, 2, 4, 5, 6, 7, 8, 9, 10, 11, 12):
+        loads[k] = pltpu.make_async_copy(far[k], near[k], load.at[k])
+        loads[k].start()
     count = [0]
 
     def copy(src, dst, target):
@@ -293,19 +303,23 @@
         return c
 
     phase("columns")
+    for k in (0, 1, 3):
+        loads[k].wait()
     mine = pl.ds(pl.multiple_of(py * 128, 128), 128)
     s1[...] = stage_columns(orb[...], sticks[0:1, mine], sticks[1:2, mine], px, ta).reshape(8, 8, 8, 128)
+    for k in (2, 4, 5, 6):
+        loads[k].wait()
     for j in range(3):
         core_out[j] = core[:, pl.ds(3 * band + j, 1)].reshape(12, N)
     for h in range(2):
         tx[h] = tyc[h].astype(F32).T.astype(BF)
     phase("barrier")
-    pl.semaphore_wait(bar, 22 + jnp.where(band != px, 1, 0))
+    pl.semaphore_wait(bar, 36 + jnp.where(band != px, 1, 0))
 
     phase("e1_y")
     flights = [copy(s1.at[ring(cy, d, 8)], r1a.at[cy], at(y=ring(cy, d, 8))) for d in range(1, 8)]
     core_copy = pltpu.make_async_remote_copy(
-        src_ref=core_out, dst_ref=core_in, send_sem=send.at[80], recv_sem=recv.at[80],
+        src_ref=core_out, dst_ref=core_in, send_sem=send.at[99], recv_sem=recv.at[99],
         device_id=swapped, device_id_type=MESH,
     )
 
@@ -345,12 +359,12 @@
             planes[r, pl.ds(pl.multiple_of(k * 16, 16), 16), :] = block[16 * r : 16 * r + 16]
         return carry
 
-    lax.fori_loop(0, 16, scatter_step, 0)
+    lax.fori_loop(0, 16, scatter_step, 0, unroll=2)
 
     phase("plane")
 
     def plane_step(j, carry):
-        rho = stage_density(planes[j], planes[3 + j], occ[0, 0], tyc, tx)
+        rho = stage_density(planes[j], planes[3 + j], occ[0], tyc, tx)
         part[j] = part[j] + stage_plane(rho, ry, rx)
         return carry
 
@@ -387,6 +401,8 @@
     for f in flights:
         f.wait()
     phase("z")
+    for k in (7, 8, 9, 10, 11, 12):
+        loads[k].wait()
     out = stage_z(r3b[...].reshape(64, 128), qx[py * 16 + px], qy[band], rz, gz)
 
     for i in range(3):
@@ -398,16 +414,13 @@
     r4a[py] = s4[py]
     for f in flights:
         f.wait()
-    phase("e4_core")
-    f = copy(r4a.at[:, :, pl.ds(pl.multiple_of(other * 8, 8), 8)], r4b.at[cc], at(c=other))
-    r4b[cc] = r4a[:, :, pl.ds(pl.multiple_of(cc * 8, 8), 8)]
-    f.wait()
     phase("e4_z")
-    flights = [
-        copy(r4b.at[:, :, :, pl.ds(ring(cz, d, 8), 1)], r4c.at[:, :, :, pl.ds(cz, 1)], at(z=ring(cz, d, 8)))
-        for d in range(1, 8)
-    ]
-    r4c[:, :, :, pl.ds(cz, 1)] = r4b[:, :, :, pl.ds(cz, 1)]
+    flights = []
+    for d in range(15, 0, -1):
+        z, c = ring(cz, d // 2, 8), lax.rem(cc + d % 2, 2)
+        rows = r4a.at[:, :, pl.ds(c * 8 + z, 1)]
+        flights.append(copy(rows, r4c.at[cc, :, :, pl.ds(cz, 1)], at(z=z, c=c)))
+    r4c[cc, :, :, pl.ds(cz, 1)] = r4a[:, :, pl.ds(cc * 8 + cz, 1)]
     for f in flights:
         f.wait()
     phase("y")
@@ -416,14 +429,12 @@
 
     s5[:, :, 0] = along.astype(BF).reshape(2, 8, 16, 128)
     s5[:, :, 1] = slope.astype(BF).reshape(2, 8, 16, 128)
-    phase("e5_y")
-    f = copy(s5.at[1 - lo], r5a.at[lo], at(y=2 * py + 1 - lo))
-    r5a[lo] = s5[lo]
-    f.wait()
-    phase("e5_x")
-    flights = [copy(r5a.at[:, ring(cx, d, 8)], r5b.at[:, cx], at(x=ring(cx, d, 8))) for d in range(1, 8)]
-    for q in range(2):
-        r5b[q, cx] = r5a[q, cx]
+    phase("e5")
+    flights = []
+    for d in range(15, 0, -1):
+        to_x, to_lo = ring(cx, d // 2, 8), lax.rem(lo + d % 2, 2)
+        flights.append(copy(s5.at[to_lo, to_x], r5b.at[lo, cx], at(x=to_x, y=2 * py + to_lo)))
+    r5b[lo, cx] = s5[lo, cx]
     for f in flights:
         f.wait()
     phase("x")
@@ -435,13 +446,31 @@
 
     r6[cc, cz] = stage_block([value, gx, gy, gzz])
     phase("e6")
-    flights = [copy(r6.at[cc, cz], r6.at[cc, cz], at(z=ring(cz, d, 8))) for d in range(1, 8)]
-    last = [copy(r6.at[cc, cz], r6.at[cc, cz], at(c=other))]
-    for d in range(1, 8):
-        flights[d - 1].wait_recv()
-        z = ring(cz, 8 - d, 8)
-        last.append(copy(r6.at[cc, z], r6.at[cc, z], at(c=other)))
-    for f in flights:
+    mine = r6.at[cc, cz]
+    hops = {d: copy(mine, mine, at(z=ring(cz, d % 8, 8))) for d in (2, -2, 1, -1)}
+    last = [copy(mine, mine, at(c=other))]
+    relays = {}
+    cut = {1: pl.ds(0, 128), -1: pl.ds(128, 112)}
+    for way in (1, -1):
+        hops[2 * way].wait_recv()
+        got = r6.at[cc, ring(cz, -2 * way % 8, 8)]
+        relays[3 * way] = copy(got, got, at(z=ring(cz, way % 8, 8)))
+        part4 = got.at[cut[way]]
+        relays[4 * way] = copy(part4, part4, at(z=ring(cz, 2 * way % 8, 8)))
+        last.append(copy(got, got, at(c=other)))
+    for way in (1, -1):
+        hops[way].wait_recv()
+        got = r6.at[cc, ring(cz, -way % 8, 8)]
+        last.append(copy(got, got, at(c=other)))
+    for way in (1, -1):
+        relays[3 * way].wait_recv()
+        got = r6.at[cc, ring(cz, -3 * way % 8, 8)]
+        last.append(copy(got, got, at(c=other)))
+    for way in (1, -1):
+        relays[4 * way].wait_recv()
+    got = r6.at[cc, ring(cz, 4, 8)]
+    last.append(copy(got, got, at(c=other)))
+    for f in list(hops.values()) + list(relays.values()):
         f.wait_send()
     for f in last:
         f.wait()
@@ -469,7 +498,8 @@
 def body(orbitals, occupations, stick_map, core_density):
     tables = make_tables()
     vmem = pl.BlockSpec(memory_space=pltpu.VMEM)
-    scratch = [
+    operands = [orbitals[0], stick_map, core_density.transpose(1, 0, 2), *tables]
+    scratch = [pltpu.VMEM(a.shape, a.dtype) for a in operands] + [
         pltpu.VMEM((2, 512, 256), BF),
         pltpu.VMEM((8, 8, 8, 128), BF),
         pltpu.VMEM((8, 8, 8, 128), BF),
@@ -487,23 +517,21 @@
         pltpu.VMEM((4, 3, 16, 128), F32),
         pltpu.VMEM((4, 3, 16, 128), F32),
         pltpu.VMEM((2, 4, 3, 8, 128), F32),
-        pltpu.VMEM((2, 4, 3, 8, 128), F32),
-        pltpu.VMEM((2, 8, 2, 16, 128), BF),
         pltpu.VMEM((2, 8, 2, 16, 128), BF),
         pltpu.VMEM((2, 8, 2, 16, 128), BF),
         pltpu.VMEM((512, 128), F32),
-        pltpu.SemaphoreType.DMA((82,)),
-        pltpu.SemaphoreType.DMA((82,)),
+        pltpu.SemaphoreType.DMA((100,)),
+        pltpu.SemaphoreType.DMA((100,)),
+        pltpu.SemaphoreType.DMA((13,)),
     ]
     blocks = pl.pallas_call(
         kernel,
         out_shape=jax.ShapeDtypeStruct((2, 8, 240, 128), BF),
-        in_specs=[vmem, pl.BlockSpec(memory_space=pltpu.SMEM), vmem, vmem]
-        + [vmem] * len(tables),
+        in_specs=[pl.BlockSpec(memory_space=pltpu.SMEM)] + [pl.BlockSpec(memory_space=pltpu.HBM)] * len(operands),
         out_specs=vmem,
         scratch_shapes=scratch,
-        compiler_params=pltpu.CompilerParams(collective_id=0, has_side_effects=True, vmem_limit_bytes=40 * 1024 * 1024),
-    )(orbitals[0], occupations.reshape(1, 1), stick_map, core_density.transpose(1, 0, 2), *tables)
+        compiler_params=pltpu.CompilerParams(collective_id=0, has_side_effects=True, vmem_limit_bytes=67_043_328),
+    )(occupations, *operands)
     pot, grad = pl.pallas_call(
         lay_kernel,
         out_shape=(

time: 118 us -> 100 us (0.85)
  local copies, waits for them, and re-layouts: 12 us -> 1.19 us
  Pallas kernels: 104 us -> 97.7 us
    unnamed x26 -> x2, local copies, waits for them, and re-layouts: 12 us -> 1.19 us
    pallas_call x1, Pallas kernels: 101 us -> 95 us  [body(): pl.pallas_call(kernel, out_shape=jax.ShapeDtypeStruct((2, 8, 240, 128), B...]
where the time goes in v2:
time: 100 us
  Pallas kernels  97.7 us (98%)
  between operations  1.29 us (1%)
  local copies, waits for them, and re-layouts  1.19 us (1%)
    pallas_call x1, Pallas kernels, body(): pl.pallas_call(kernel, out_shape=jax.ShapeDtypeStruct((2, 8, 240, 128), B...  95 us
    pallas_call x1, Pallas kernels, body(): pl.pallas_call(lay_kernel, out_shape=(jax.ShapeDtypeStruct((12, 48, N), F...  2.67 us

profile of v2, /device:TPU:1, one launch (start us, length us, event | category | flops | bytes accessed | tf_op | source)
XLA Modules:
  0.0 100.2 jit_solution(16245302109670279471)
XLA Ops:
  1.3 95.0 %shard_map.149.r6 = bf16[2,8,240,128]{3,2,1,0:T(8,128)(2,1)} custom-call(f32[1]{0:T(128)S(6)} %copy.16.occ, bf16[128,384]{1,0:T(8,128)(2,1)} %bitcast.5, s32[2,512]{1,0:T(2,128)} %rest_1_.1, f32[12,48,192]{2,1,0:T(8,128)} %bitcast.4, bf16[2,512,384]{2,1,0:T(8,128)(2,1)} %constant.20.clone.rest_3_, bf16[2,256,512]{2,1,0:T(8,128)(2,1)} %constant.21.clone.rest_4_, ...), custom_call_target="tpu_custom_call" | custom-call | tf_op jit(solution)/shard_map/pallas_call | solution.py:527
  96.3 0.0 copy-start
  96.3 1.2 %copy-done = bf16[2,8,240,128]{3,2,1,0:T(8,128)(2,1)S(1)} copy-done((bf16[2,8,240,128]{3,2,1,0:T(8,128)(2,1)S(1)}, bf16[2,8,240,128]{3,2,1,0:T(8,128)(2,1)}, u32[]{:S(2)}) %copy-start) | copy-done | bytes 983064
  97.5 2.7 %shard_map.150 = (f32[12,48,192]{2,1,0:T(8,128)}, f32[3,12,48,192]{3,2,1,0:T(8,128)}) custom-call(bf16[2,8,240,128]{3,2,1,0:T(8,128)(2,1)S(1)} %copy-done), custom_call_target="tpu_custom_call" | custom-call | tf_op jit(solution)/shard_map/pallas_call | solution.py:535
Async XLA Ops:
  96.3 1.2 %copy-start = (bf16[2,8,240,128]{3,2,1,0:T(8,128)(2,1)S(1)}, bf16[2,8,240,128]{3,2,1,0:T(8,128)(2,1)}, u32[]{:S(2)}) copy-start(bf16[2,8,240,128]{3,2,1,0:T(8,128)(2,1)} %shard_map.149.r6) | copy-start | bytes 2949124

commit v3 on v2

--- a/solution.py
+++ b/solution.py
@@ -124,15 +124,25 @@
     return mmt(rows.astype(BF), hot).astype(BF)
 
 
-def stage_density(p_re, p_im, weight, tyc, tx):
-    a = mm(p_re, tyc[0]) + mm(p_re, tyc[1])
-    b = mm(p_im, tyc[0]) + mm(p_im, tyc[1])
-    y_re = (a[:, :256] - b[:, 256:]).astype(BF)
-    y_im = (a[:, 256:] + b[:, :256]).astype(BF)
-    a = mm(tx[0], y_re) + mm(tx[1], y_re)
-    b = mm(tx[0], y_im) + mm(tx[1], y_im)
-    re = a[:N] - b[256 : 256 + N]
-    im = a[256 : 256 + N] + b[:N]
+def stage_tables(tyc, ty, tx):
+    for h in range(2):
+        c, s = tyc[h, :, :256], tyc[h, :, 256:]
+        ty[512 * h : 512 * h + 256, 0:256] = c
+        ty[512 * h : 512 * h + 256, 256:512] = s
+        ty[512 * h + 256 : 512 * h + 512, 0:256] = -s
+        ty[512 * h + 256 : 512 * h + 512, 256:512] = c
+        ct, st = (t.astype(F32).T[:N].astype(BF) for t in (c, s))
+        tx[0:N, 512 * h : 512 * h + 256] = ct
+        tx[0:N, 512 * h + 256 : 512 * h + 512] = -st
+        tx[N : 2 * N, 512 * h : 512 * h + 256] = st
+        tx[N : 2 * N, 512 * h + 256 : 512 * h + 512] = ct
+
+
+def stage_density(p_re, p_im, weight, ty, tx):
+    along = mm(jnp.concatenate([p_re, p_im, p_re, p_im], axis=1), ty[...]).astype(BF)
+    rows = jnp.concatenate([along[:, :256], along[:, 256:]], axis=0)
+    both = mm(tx[...], jnp.concatenate([rows, rows], axis=0))
+    re, im = both[:N], both[N:]
     return weight * (re * re + im * im)
 
 
@@ -243,7 +253,7 @@
     r6, near, rest = rest[0], rest[1:14], rest[14:]
     orb, sticks, core, ta, tyc, ry, rx, rz, gz, ryi, rxi, qx, qy = near
     (
-    tx, s1, r1a, r1b, core_out, core_in, planes, part, r2a, sums, r2b, s3, r3a, r3b, s4, r4a, r4c,
+    ty, tx, s1, r1a, r1b, core_out, core_in, planes, part, r2a, sums, r2b, s3, r3a, r3b, s4, r4a, r4c,
     s5, r5b, wide, send, recv, load,
     ) = rest
     band, px, py = lax.axis_index("band"), lax.axis_index("px"), lax.axis_index("py")
@@ -307,19 +317,16 @@
         loads[k].wait()
     mine = pl.ds(pl.multiple_of(py * 128, 128), 128)
     s1[...] = stage_columns(orb[...], sticks[0:1, mine], sticks[1:2, mine], px, ta).reshape(8, 8, 8, 128)
-    for k in (2, 4, 5, 6):
-        loads[k].wait()
+    loads[2].wait()
     for j in range(3):
         core_out[j] = core[:, pl.ds(3 * band + j, 1)].reshape(12, N)
-    for h in range(2):
-        tx[h] = tyc[h].astype(F32).T.astype(BF)
     phase("barrier")
     pl.semaphore_wait(bar, 36 + jnp.where(band != px, 1, 0))
 
     phase("e1_y")
     flights = [copy(s1.at[ring(cy, d, 8)], r1a.at[cy], at(y=ring(cy, d, 8))) for d in range(1, 8)]
     core_copy = pltpu.make_async_remote_copy(
-        src_ref=core_out, dst_ref=core_in, send_sem=send.at[99], recv_sem=recv.at[99],
+        src_ref=core_out, dst_ref=core_in, send_sem=send.at[119], recv_sem=recv.at[119],
         device_id=swapped, device_id_type=MESH,
     )
 
@@ -332,6 +339,9 @@
         core_in[...] = core_out[...]
 
     r1a[cy] = s1[cy]
+    for k in (4, 5, 6):
+        loads[k].wait()
+    stage_tables(tyc, ty, tx)
     for f in flights:
         f.wait()
     phase("e1_x_core")
@@ -348,38 +358,56 @@
         return carry
 
     lax.fori_loop(0, 3, core_step, 0)
-    phase("e1_x_wait")
-    for f in flights:
-        f.wait()
-
     phase("scatter")
-    def scatter_step(k, carry):
-        block = stage_scatter([r1b[2 * q + k // 8, k % 8] for q in range(4)])
-        for r in range(6):
-            planes[r, pl.ds(pl.multiple_of(k * 16, 16), 16), :] = block[16 * r : 16 * r + 16]
+    arrival = count[0] - 8
+
+    def scatter_step(q, carry):
+        odd = q % 2
+        d = odd * ((q + 1) // 2) + (1 - odd) * (8 - q // 2)
+        source = lax.rem(cx + 8 - d, 8)
+
+        @pl.when(q > 0)
+        def _():
+            pltpu.make_async_remote_copy(
+                src_ref=r1a.at[:, source], dst_ref=r1b.at[:, source],
+                send_sem=send.at[arrival + d], recv_sem=recv.at[arrival + d],
+                device_id=at(x=source), device_id_type=MESH,
+            ).wait_recv()
+
+        for l in range(2):
+            block = stage_scatter([r1b[2 * q4 + l, source] for q4 in range(4)])
+            row = pl.ds(pl.multiple_of(128 * l + source * 16, 16), 16)
+            for r in range(6):
+                planes[r, row, :] = block[16 * r : 16 * r + 16]
         return carry
 
-    lax.fori_loop(0, 16, scatter_step, 0, unroll=2)
-
-    phase("plane")
-
-    def plane_step(j, carry):
-        rho = stage_density(planes[j], planes[3 + j], occ[0], tyc, tx)
-        part[j] = part[j] + stage_plane(rho, ry, rx)
-        return carry
-
-    lax.fori_loop(0, 3, plane_step, 0)
-
-    phase("e2_core")
+    lax.fori_loop(0, 8, scatter_step, 0)
+    for f in flights:
+        f.wait_send()
+
     other = 1 - cc
-    f = copy(part.at[:, pl.ds(pl.multiple_of(other * 128, 128), 128)], r2a, at(c=other))
-    f.wait()
-    for j in range(3):
+    flights, pairs = [], []
+
+    def spread(j):
+        pairs[j].wait()
         total = part[j, pl.ds(pl.multiple_of(cc * 128, 128), 128)] + r2a[j]
         sums[j] = halves_for_wire(total).reshape(8, 16, 256)
+        for d in (4, 3, 5, 2, 6, 1, 7):
+            z = ring(cz, d, 8)
+            flights.append(copy(sums.at[j, z], r2b.at[cz, j], at(z=z)))
+        r2b[cz, j] = sums[j, cz]
+
+    for j in range(3):
+        phase(f"plane{j}")
+        rho = stage_density(planes[j], planes[3 + j], occ[0], ty, tx)
+        part[j] = part[j] + stage_plane(rho, ry, rx)
+        pairs.append(copy(part.at[j, pl.ds(pl.multiple_of(other * 128, 128), 128)], r2a.at[j], at(c=other)))
+        if j > 0:
+            phase(f"spread{j}")
+            spread(j - 1)
+    phase("spread3")
+    spread(2)
     phase("e2_z")
-    flights = [copy(sums.at[:, ring(cz, d, 8)], r2b.at[cz], at(z=ring(cz, d, 8))) for d in range(1, 8)]
-    r2b[cz] = sums[:, cz]
     for f in flights:
         f.wait()
     acc = r2b[0].astype(F32)
@@ -477,30 +505,44 @@
     phase(None)
 
 
-def lay_kernel(r6, pot, grad, wide, woven):
-    wide[...] = r6[...].astype(F32).reshape(3840, 128)
+def lay_kernel(r6, pot, grad, got, wide, woven, done, load, store):
+    loads = [pltpu.make_async_copy(r6.at[c], got.at[c], load.at[c]) for c in range(2)]
+    for c in loads:
+        c.start()
+    for c in range(2):
+        loads[c].wait()
+        wide[1920 * c : 1920 * c + 1920] = got[c].astype(F32).reshape(1920, 128)
 
     def step(y, carry):
         for k in range(4):
-            ref = pot.at[y] if k == 0 else grad.at[k - 1, y]
             for j in range(3):
                 z = pl.ds(j, 16, stride=3)
                 woven[k, 0, z] = wide[pl.ds(40 * k + 12 * j + y, 16, stride=240), :]
                 tail = wide[pl.ds(160 + 40 * (k // 2) + 12 * j + y, 16, stride=240), :]
                 woven[k, 1, z] = roll(tail, 64, 1) if k % 2 else tail
-            ref[:, 0:128] = woven[k, 0]
-            ref[:, 128:192] = woven[k, 1, :, 0:64]
+            done[k, y, :, 0:128] = woven[k, 0]
+            done[k, y, :, 128:192] = woven[k, 1, :, 0:64]
         return carry
 
-    lax.fori_loop(0, 12, step, 0)
+    stores = []
+    for q in range(3):
+        lax.fori_loop(4 * q, 4 * q + 4, step, 0)
+        rows = pl.ds(4 * q, 4)
+        for k in range(4):
+            target = pot.at[rows] if k == 0 else grad.at[k - 1, rows]
+            stores.append(pltpu.make_async_copy(done.at[k, rows], target, store.at[4 * q + k]))
+            stores[-1].start()
+    for c in stores:
+        c.wait()
 
 
 def body(orbitals, occupations, stick_map, core_density):
     tables = make_tables()
-    vmem = pl.BlockSpec(memory_space=pltpu.VMEM)
+    far = pl.BlockSpec(memory_space=pltpu.HBM)
     operands = [orbitals[0], stick_map, core_density.transpose(1, 0, 2), *tables]
     scratch = [pltpu.VMEM(a.shape, a.dtype) for a in operands] + [
-        pltpu.VMEM((2, 512, 256), BF),
+        pltpu.VMEM((1024, 512), BF),
+        pltpu.VMEM((384, 1024), BF),
         pltpu.VMEM((8, 8, 8, 128), BF),
         pltpu.VMEM((8, 8, 8, 128), BF),
         pltpu.VMEM((8, 8, 8, 128), BF),
@@ -520,15 +562,15 @@
         pltpu.VMEM((2, 8, 2, 16, 128), BF),
         pltpu.VMEM((2, 8, 2, 16, 128), BF),
         pltpu.VMEM((512, 128), F32),
-        pltpu.SemaphoreType.DMA((100,)),
-        pltpu.SemaphoreType.DMA((100,)),
+        pltpu.SemaphoreType.DMA((120,)),
+        pltpu.SemaphoreType.DMA((120,)),
         pltpu.SemaphoreType.DMA((13,)),
     ]
     blocks = pl.pallas_call(
         kernel,
         out_shape=jax.ShapeDtypeStruct((2, 8, 240, 128), BF),
-        in_specs=[pl.BlockSpec(memory_space=pltpu.SMEM)] + [pl.BlockSpec(memory_space=pltpu.HBM)] * len(operands),
-        out_specs=vmem,
+        in_specs=[pl.BlockSpec(memory_space=pltpu.SMEM)] + [far] * len(operands),
+        out_specs=pl.BlockSpec(memory_space=pltpu.VMEM),
         scratch_shapes=scratch,
         compiler_params=pltpu.CompilerParams(collective_id=0, has_side_effects=True, vmem_limit_bytes=67_043_328),
     )(occupations, *operands)
@@ -538,10 +580,17 @@
             jax.ShapeDtypeStruct((12, 48, N), F32),
             jax.ShapeDtypeStruct((3, 12, 48, N), F32),
         ),
-        in_specs=[vmem],
-        out_specs=(vmem, vmem),
-        scratch_shapes=[pltpu.VMEM((3840, 128), F32), pltpu.VMEM((4, 2, 48, 128), F32)],
-        compiler_params=pltpu.CompilerParams(vmem_limit_bytes=20 * 1024 * 1024),
+        in_specs=[far],
+        out_specs=(far, far),
+        scratch_shapes=[
+            pltpu.VMEM((2, 8, 240, 128), BF),
+            pltpu.VMEM((3840, 128), F32),
+            pltpu.VMEM((4, 2, 48, 128), F32),
+            pltpu.VMEM((4, 12, 48, N), F32),
+            pltpu.SemaphoreType.DMA((2,)),
+            pltpu.SemaphoreType.DMA((12,)),
+        ],
+        compiler_params=pltpu.CompilerParams(vmem_limit_bytes=67_043_328),
     )(blocks)
     return pot.transpose(1, 0, 2), grad.transpose(0, 2, 1, 3)
 

time: 100 us -> 95.6 us (0.956)
  Pallas kernels: 97.7 us -> 94.1 us
  local copies, waits for them, and re-layouts: 1.19 us -> 0 us
    pallas_call x1, Pallas kernels: 95 us -> 90.7 us  [body(): pl.pallas_call(kernel, out_shape=jax.ShapeDtypeStruct((2, 8, 240, 128), B...]
    unnamed x2 -> x0, local copies, waits for them, and re-layouts: 1.19 us -> none
where the time goes in v3:
time: 95.6 us; the launch traced here: 95.4 us
  Pallas kernels  94.1 us (98%)
  between operations  1.28 us (1%)
    pallas_call x1, Pallas kernels, body(): pl.pallas_call(kernel, out_shape=jax.ShapeDtypeStruct((2, 8, 240, 128), B...  90.7 us
    pallas_call x1, Pallas kernels, body(): pl.pallas_call(lay_kernel, out_shape=(jax.ShapeDtypeStruct((12, 48, N), F...  3.4 us

profile of v3, /device:TPU:1, one launch (start us, length us, event | category | flops | bytes accessed | tf_op | source)
XLA Modules:
  0.0 95.4 jit_solution(7412006005662736171)
XLA Ops:
  1.3 90.7 %shard_map.149.r6 = bf16[2,8,240,128]{3,2,1,0:T(8,128)(2,1)} custom-call(f32[1]{0:T(128)S(6)} %copy.16.occ, bf16[128,384]{1,0:T(8,128)(2,1)} %bitcast.5, s32[2,512]{1,0:T(2,128)} %rest_1_.1, f32[12,48,192]{2,1,0:T(8,128)} %bitcast.4, bf16[2,512,384]{2,1,0:T(8,128)(2,1)} %constant.20.clone.rest_3_, bf16[2,256,512]{2,1,0:T(8,128)(2,1)} %constant.21.clone.rest_4_, ...), custom_call_target="tpu_custom_call" | custom-call | tf_op jit(solution)/shard_map/pallas_call | solution.py:569
  92.0 3.4 %shard_map.150 = (f32[12,48,192]{2,1,0:T(8,128)}, f32[3,12,48,192]{3,2,1,0:T(8,128)}) custom-call(bf16[2,8,240,128]{3,2,1,0:T(8,128)(2,1)} %shard_map.149.r6), custom_call_target="tpu_custom_call" | custom-call | tf_op jit(solution)/shard_map/pallas_call | solution.py:577

commit v4 on v3

--- a/solution.py
+++ b/solution.py
@@ -19,6 +19,7 @@
 F32 = jnp.float32
 BF = jnp.bfloat16
 MESH = pl.DeviceIdType.MESH
+FAR_FIRST = (4, 3, 5, 2, 6, 1, 7)
 roll = pltpu.roll
 
 
@@ -215,7 +216,14 @@
 
 def stage_y(x, ryi):
     cols = split(jnp.concatenate(swap_minor(x), axis=0))
-    return mm3((ryi[0][0], ryi[1][0]), cols), mm3((ryi[0][1], ryi[1][1]), cols)
+    along, slope = mm3((ryi[0][0], ryi[1][0]), cols), mm3((ryi[0][1], ryi[1][1]), cols)
+    row = lax.broadcasted_iota(jnp.int32, (256, 128), 0) % 16
+    lane = lax.broadcasted_iota(jnp.int32, (256, 128), 1)
+    spare = roll(jnp.where(lane < 36, slope, 0.0), 12, 0)
+    for h in (1, 2):
+        moved = roll(roll(slope, 12 - 4 * h, 0), 40 * h, 1)
+        spare = jnp.where((lane >= 40 * h) & (lane < 40 * h + 36), moved, spare)
+    return jnp.where(row < 12, along, spare)
 
 
 def stage_x(a, g, rxi):
@@ -250,11 +258,11 @@
     occ, *rest,
 ):
     far, rest = rest[:13], rest[13:]
-    r6, near, rest = rest[0], rest[1:14], rest[14:]
+    out, near, rest = rest[0], rest[1:14], rest[14:]
     orb, sticks, core, ta, tyc, ry, rx, rz, gz, ryi, rxi, qx, qy = near
     (
     ty, tx, s1, r1a, r1b, core_out, core_in, planes, part, r2a, sums, r2b, s3, r3a, r3b, s4, r4a, r4c,
-    s5, r5b, wide, send, recv, load,
+    s5, r5b, wide, r6, send, recv, load, store,
     ) = rest
     band, px, py = lax.axis_index("band"), lax.axis_index("px"), lax.axis_index("py")
     cz, cc = band // 2, band % 2
@@ -302,9 +310,10 @@
         loads[k].start()
     count = [0]
 
-    def copy(src, dst, target):
-        k = count[0]
-        count[0] += 1
+    def copy(src, dst, target, k=None):
+        if k is None:
+            k = count[0]
+            count[0] += 1
         c = pltpu.make_async_remote_copy(
             src_ref=src, dst_ref=dst, send_sem=send.at[k], recv_sem=recv.at[k],
             device_id=target, device_id_type=MESH,
@@ -324,7 +333,7 @@
     pl.semaphore_wait(bar, 36 + jnp.where(band != px, 1, 0))
 
     phase("e1_y")
-    flights = [copy(s1.at[ring(cy, d, 8)], r1a.at[cy], at(y=ring(cy, d, 8))) for d in range(1, 8)]
+    flights = [copy(s1.at[ring(cy, d, 8)], r1a.at[cy], at(y=ring(cy, d, 8))) for d in FAR_FIRST]
     core_copy = pltpu.make_async_remote_copy(
         src_ref=core_out, dst_ref=core_in, send_sem=send.at[119], recv_sem=recv.at[119],
         device_id=swapped, device_id_type=MESH,
@@ -345,7 +354,11 @@
     for f in flights:
         f.wait()
     phase("e1_x_core")
-    flights = [copy(r1a.at[:, ring(cx, d, 8)], r1b.at[:, cx], at(x=ring(cx, d, 8))) for d in range(1, 8)]
+    arrival = count[0] - 1
+    flights = [
+        copy(r1a.at[:, ring(cx, d, 8)], r1b.at[:, cx], at(x=ring(cx, d, 8)), arrival + d) for d in FAR_FIRST
+    ]
+    count[0] += 7
     for y in range(8):
         r1b[y, cx] = r1a[y, cx]
 
@@ -359,8 +372,6 @@
 
     lax.fori_loop(0, 3, core_step, 0)
     phase("scatter")
-    arrival = count[0] - 8
-
     def scatter_step(q, carry):
         odd = q % 2
         d = odd * ((q + 1) // 2) + (1 - odd) * (8 - q // 2)
@@ -392,7 +403,7 @@
         pairs[j].wait()
         total = part[j, pl.ds(pl.multiple_of(cc * 128, 128), 128)] + r2a[j]
         sums[j] = halves_for_wire(total).reshape(8, 16, 256)
-        for d in (4, 3, 5, 2, 6, 1, 7):
+        for d in FAR_FIRST:
             z = ring(cz, d, 8)
             flights.append(copy(sums.at[j, z], r2b.at[cz, j], at(z=z)))
         r2b[cz, j] = sums[j, cz]
@@ -417,13 +428,13 @@
     phase("pack")
     s3[...] = stage_pack(acc).reshape(8, 8, 128)
     phase("e3_y")
-    flights = [copy(s3.at[ring(cy, d, 8)], r3a.at[cy], at(y=ring(cy, d, 8))) for d in range(1, 8)]
+    flights = [copy(s3.at[ring(cy, d, 8)], r3a.at[cy], at(y=ring(cy, d, 8))) for d in FAR_FIRST]
     r3a[cy] = s3[cy]
     for f in flights:
         f.wait()
     phase("e3_x")
     flights = [
-        copy(r3a.at[:, pl.ds(ring(cx, d, 8), 1)], r3b.at[:, pl.ds(cx, 1)], at(x=ring(cx, d, 8))) for d in range(1, 8)
+        copy(r3a.at[:, pl.ds(ring(cx, d, 8), 1)], r3b.at[:, pl.ds(cx, 1)], at(x=ring(cx, d, 8))) for d in FAR_FIRST
     ]
     r3b[:, pl.ds(cx, 1)] = r3a[:, pl.ds(cx, 1)]
     for f in flights:
@@ -431,10 +442,10 @@
     phase("z")
     for k in (7, 8, 9, 10, 11, 12):
         loads[k].wait()
-    out = stage_z(r3b[...].reshape(64, 128), qx[py * 16 + px], qy[band], rz, gz)
+    turned = stage_z(r3b[...].reshape(64, 128), qx[py * 16 + px], qy[band], rz, gz)
 
     for i in range(3):
-        s4[:, i] = out[i].reshape(4, 16, 128)
+        s4[:, i] = turned[i].reshape(4, 16, 128)
     phase("e4_y")
     flights = [
         copy(s4.at[ring(py, d, 4)], r4a.at[py], at(y=2 * ring(py, d, 4) + lo)) for d in range(1, 4)
@@ -444,8 +455,8 @@
         f.wait()
     phase("e4_z")
     flights = []
-    for d in range(15, 0, -1):
-        z, c = ring(cz, d // 2, 8), lax.rem(cc + d % 2, 2)
+    for d, flip in [(d, flip) for d in FAR_FIRST for flip in (1, 0)] + [(0, 1)]:
+        z, c = ring(cz, d, 8), lax.rem(cc + flip, 2)
         rows = r4a.at[:, :, pl.ds(c * 8 + z, 1)]
         flights.append(copy(rows, r4c.at[cc, :, :, pl.ds(cz, 1)], at(z=z, c=c)))
     r4c[cc, :, :, pl.ds(cz, 1)] = r4a[:, :, pl.ds(cc * 8 + cz, 1)]
@@ -453,54 +464,74 @@
         f.wait()
     phase("y")
     x = [jnp.concatenate([r4c[0, q, i], r4c[1, q, i]], axis=0) for i in range(3) for q in range(4)]
-    along, slope = stage_y(x, ryi)
-
-    s5[:, :, 0] = along.astype(BF).reshape(2, 8, 16, 128)
-    s5[:, :, 1] = slope.astype(BF).reshape(2, 8, 16, 128)
+    along = stage_y(x, ryi)
+
+    s5[...] = along.astype(BF).reshape(2, 8, 16, 128)
     phase("e5")
     flights = []
-    for d in range(15, 0, -1):
-        to_x, to_lo = ring(cx, d // 2, 8), lax.rem(lo + d % 2, 2)
+    for d, flip in [(d, flip) for d in FAR_FIRST for flip in (1, 0)] + [(0, 1)]:
+        to_x, to_lo = ring(cx, d, 8), lax.rem(lo + flip, 2)
         flights.append(copy(s5.at[to_lo, to_x], r5b.at[lo, cx], at(x=to_x, y=2 * py + to_lo)))
     r5b[lo, cx] = s5[lo, cx]
     for f in flights:
         f.wait()
     phase("x")
-    wide[...] = r5b[...].astype(F32).reshape(512, 128)
-    a = [wide[pl.ds(y, 16, stride=32), :] for y in range(12)]
-    g = [wide[pl.ds(16 + y, 16, stride=32), :] for y in range(12)]
-    rho, hart, gx, gy, gzz = stage_x(a, g, rxi)
+    wide[...] = r5b[...].astype(F32).reshape(256, 128)
+    a = [wide[pl.ds(y, 16, stride=16), :] for y in range(16)]
+    g = [a[12 + y % 4] if y < 4 else roll(a[12 + y % 4], 128 - 40 * (y // 4), 1) for y in range(12)]
+    rho, hart, gx, gy, gzz = stage_x(a[:12], g, rxi)
     value = stage_potential(rho, hart, gx, gy, gzz)
 
     r6[cc, cz] = stage_block([value, gx, gy, gzz])
     phase("e6")
-    mine = r6.at[cc, cz]
-    hops = {d: copy(mine, mine, at(z=ring(cz, d % 8, 8))) for d in (2, -2, 1, -1)}
-    last = [copy(mine, mine, at(c=other))]
-    relays = {}
-    cut = {1: pl.ds(0, 128), -1: pl.ds(128, 112)}
+    chunks = (pl.ds(0, 128), pl.ds(128, 112))
+    hops, relays, last, home = {}, {}, [], []
+
+    def block(away):
+        return r6.at[cc, ring(cz, away % 8, 8)]
+
+    def go(ref, away):
+        return copy(ref, ref, at(z=ring(cz, away % 8, 8)))
+
+    def settle(away):
+        last.append(copy(block(away), block(away), at(c=other)))
+        for c in (cc, other):
+            k = len(home)
+            ref = (c, ring(cz, away % 8, 8))
+            home.append(pltpu.make_async_copy(r6.at[ref], out.at[ref], store.at[k]))
+        home[-2].start()
+
+    for d in (2, -2):
+        for h in (0, 1):
+            hops[d, h] = go(block(0).at[chunks[h]], d)
+    for d in (1, -1):
+        hops[d, 0] = go(block(0), d)
+    settle(0)
+    for h in (0, 1):
+        for way in (1, -1):
+            hops[2 * way, h].wait_recv()
+            got = block(-2 * way).at[chunks[h]]
+            relays[3 * way, h] = go(got, way)
+            if h == (1 - way) // 2:
+                relays[4 * way, h] = go(got, 2 * way)
+    settle(-2)
+    settle(2)
     for way in (1, -1):
-        hops[2 * way].wait_recv()
-        got = r6.at[cc, ring(cz, -2 * way % 8, 8)]
-        relays[3 * way] = copy(got, got, at(z=ring(cz, way % 8, 8)))
-        part4 = got.at[cut[way]]
-        relays[4 * way] = copy(part4, part4, at(z=ring(cz, 2 * way % 8, 8)))
-        last.append(copy(got, got, at(c=other)))
+        hops[way, 0].wait_recv()
+        settle(-way)
     for way in (1, -1):
-        hops[way].wait_recv()
-        got = r6.at[cc, ring(cz, -way % 8, 8)]
-        last.append(copy(got, got, at(c=other)))
-    for way in (1, -1):
-        relays[3 * way].wait_recv()
-        got = r6.at[cc, ring(cz, -3 * way % 8, 8)]
-        last.append(copy(got, got, at(c=other)))
-    for way in (1, -1):
-        relays[4 * way].wait_recv()
-    got = r6.at[cc, ring(cz, 4, 8)]
-    last.append(copy(got, got, at(c=other)))
+        for h in (0, 1):
+            relays[3 * way, h].wait_recv()
+        settle(-3 * way)
+    relays[4, 0].wait_recv()
+    relays[-4, 1].wait_recv()
+    settle(4)
+    for k in range(8):
+        last[k].wait()
+        home[2 * k + 1].start()
     for f in list(hops.values()) + list(relays.values()):
         f.wait_send()
-    for f in last:
+    for f in home:
         f.wait()
     phase(None)
 
@@ -559,18 +590,20 @@
         pltpu.VMEM((4, 3, 16, 128), F32),
         pltpu.VMEM((4, 3, 16, 128), F32),
         pltpu.VMEM((2, 4, 3, 8, 128), F32),
-        pltpu.VMEM((2, 8, 2, 16, 128), BF),
-        pltpu.VMEM((2, 8, 2, 16, 128), BF),
-        pltpu.VMEM((512, 128), F32),
+        pltpu.VMEM((2, 8, 16, 128), BF),
+        pltpu.VMEM((2, 8, 16, 128), BF),
+        pltpu.VMEM((256, 128), F32),
+        pltpu.VMEM((2, 8, 240, 128), BF),
         pltpu.SemaphoreType.DMA((120,)),
         pltpu.SemaphoreType.DMA((120,)),
         pltpu.SemaphoreType.DMA((13,)),
+        pltpu.SemaphoreType.DMA((16,)),
     ]
     blocks = pl.pallas_call(
         kernel,
         out_shape=jax.ShapeDtypeStruct((2, 8, 240, 128), BF),
         in_specs=[pl.BlockSpec(memory_space=pltpu.SMEM)] + [far] * len(operands),
-        out_specs=pl.BlockSpec(memory_space=pltpu.VMEM),
+        out_specs=far,
         scratch_shapes=scratch,
         compiler_params=pltpu.CompilerParams(collective_id=0, has_side_effects=True, vmem_limit_bytes=67_043_328),
     )(occupations, *operands)

time: 95.6 us -> 93.1 us (0.974)
  Pallas kernels: 94.1 us -> 91.6 us
    pallas_call x1, Pallas kernels: 90.7 us -> 88.2 us  [body(): pl.pallas_call(kernel, out_shape=jax.ShapeDtypeStruct((2, 8, 240, 128), B...]
where the time goes in v4:
time: 93.1 us; the launch traced here: 92.9 us
  Pallas kernels  91.6 us (98%)
  between operations  1.28 us (1%)
    pallas_call x1, Pallas kernels, body(): pl.pallas_call(kernel, out_shape=jax.ShapeDtypeStruct((2, 8, 240, 128), B...  88.2 us
    pallas_call x1, Pallas kernels, body(): pl.pallas_call(lay_kernel, out_shape=(jax.ShapeDtypeStruct((12, 48, N), F...  3.4 us

profile of v4, /device:TPU:1, one launch (start us, length us, event | category | flops | bytes accessed | tf_op | source)
XLA Modules:
  0.0 92.9 jit_solution(14869245998895847925)
XLA Ops:
  1.3 88.2 %shard_map.149.r6 = bf16[2,8,240,128]{3,2,1,0:T(8,128)(2,1)} custom-call(f32[1]{0:T(128)S(6)} %copy.16.occ, bf16[128,384]{1,0:T(8,128)(2,1)} %bitcast.5, s32[2,512]{1,0:T(2,128)} %rest_1_.1, f32[12,48,192]{2,1,0:T(8,128)} %bitcast.4, bf16[2,512,384]{2,1,0:T(8,128)(2,1)} %constant.20.clone.rest_3_, bf16[2,256,512]{2,1,0:T(8,128)(2,1)} %constant.21.clone.rest_4_, ...), custom_call_target="tpu_custom_call" | custom-call | tf_op jit(solution)/shard_map/pallas_call | solution.py:602
  89.5 3.4 %shard_map.150 = (f32[12,48,192]{2,1,0:T(8,128)}, f32[3,12,48,192]{3,2,1,0:T(8,128)}) custom-call(bf16[2,8,240,128]{3,2,1,0:T(8,128)(2,1)} %shard_map.149.r6), custom_call_target="tpu_custom_call" | custom-call | tf_op jit(solution)/shard_map/pallas_call | solution.py:610

commit v5 on v4

--- a/solution.py
+++ b/solution.py
@@ -261,7 +261,7 @@
     out, near, rest = rest[0], rest[1:14], rest[14:]
     orb, sticks, core, ta, tyc, ry, rx, rz, gz, ryi, rxi, qx, qy = near
     (
-    ty, tx, s1, r1a, r1b, core_out, core_in, planes, part, r2a, sums, r2b, s3, r3a, r3b, s4, r4a, r4c,
+    ty, tx, s1, r1a, r1b, core_out, core_in, planes, part, r2a, sums, r2b, s3, r3a, r3b, s4, r4c,
     s5, r5b, wide, r6, send, recv, load, store,
     ) = rest
     band, px, py = lax.axis_index("band"), lax.axis_index("px"), lax.axis_index("py")
@@ -296,8 +296,6 @@
         hail(at(x=ring(cx, d, 8)))
         hail(at(y=ring(cy, d, 8)))
         hail(at(z=ring(cz, d, 8)))
-        hail(at(z=ring(cz, d, 8), c=1 - cc))
-        hail(at(x=ring(cx, d, 8), y=2 * py + 1 - lo))
     hail(at(c=1 - cc))
 
     @pl.when(band != px)
@@ -330,12 +328,12 @@
     for j in range(3):
         core_out[j] = core[:, pl.ds(3 * band + j, 1)].reshape(12, N)
     phase("barrier")
-    pl.semaphore_wait(bar, 36 + jnp.where(band != px, 1, 0))
+    pl.semaphore_wait(bar, 22 + jnp.where(band != px, 1, 0))
 
     phase("e1_y")
     flights = [copy(s1.at[ring(cy, d, 8)], r1a.at[cy], at(y=ring(cy, d, 8))) for d in FAR_FIRST]
     core_copy = pltpu.make_async_remote_copy(
-        src_ref=core_out, dst_ref=core_in, send_sem=send.at[119], recv_sem=recv.at[119],
+        src_ref=core_out, dst_ref=core_in, send_sem=send.at[179], recv_sem=recv.at[179],
         device_id=swapped, device_id_type=MESH,
     )
 
@@ -444,22 +442,18 @@
         loads[k].wait()
     turned = stage_z(r3b[...].reshape(64, 128), qx[py * 16 + px], qy[band], rz, gz)
 
+    phase("e4")
     for i in range(3):
         s4[:, i] = turned[i].reshape(4, 16, 128)
-    phase("e4_y")
-    flights = [
-        copy(s4.at[ring(py, d, 4)], r4a.at[py], at(y=2 * ring(py, d, 4) + lo)) for d in range(1, 4)
-    ]
-    r4a[py] = s4[py]
-    for f in flights:
-        f.wait()
-    phase("e4_z")
     flights = []
-    for d, flip in [(d, flip) for d in FAR_FIRST for flip in (1, 0)] + [(0, 1)]:
-        z, c = ring(cz, d, 8), lax.rem(cc + flip, 2)
-        rows = r4a.at[:, :, pl.ds(c * 8 + z, 1)]
-        flights.append(copy(rows, r4c.at[cc, :, :, pl.ds(cz, 1)], at(z=z, c=c)))
-    r4c[cc, :, :, pl.ds(cz, 1)] = r4a[:, :, pl.ds(cc * 8 + cz, 1)]
+    for e in (2, 1, 3, 0):
+        y = ring(py, e, 4)
+        for d, flip in [(d, flip) for d in FAR_FIRST + (0,) for flip in (1, 0)]:
+            if e or d or flip:
+                z, c = ring(cz, d, 8), lax.rem(cc + flip, 2)
+                rows = s4.at[y, :, pl.ds(c * 8 + z, 1)]
+                flights.append(copy(rows, r4c.at[cc, py, :, pl.ds(cz, 1)], at(z=z, c=c, y=2 * y + lo)))
+    r4c[cc, py, :, pl.ds(cz, 1)] = s4[py, :, pl.ds(cc * 8 + cz, 1)]
     for f in flights:
         f.wait()
     phase("y")
@@ -588,14 +582,13 @@
         pltpu.VMEM((8, 8, 128), F32),
         pltpu.VMEM((8, 8, 128), F32),
         pltpu.VMEM((4, 3, 16, 128), F32),
-        pltpu.VMEM((4, 3, 16, 128), F32),
         pltpu.VMEM((2, 4, 3, 8, 128), F32),
         pltpu.VMEM((2, 8, 16, 128), BF),
         pltpu.VMEM((2, 8, 16, 128), BF),
         pltpu.VMEM((256, 128), F32),
         pltpu.VMEM((2, 8, 240, 128), BF),
-        pltpu.SemaphoreType.DMA((120,)),
-        pltpu.SemaphoreType.DMA((120,)),
+        pltpu.SemaphoreType.DMA((180,)),
+        pltpu.SemaphoreType.DMA((180,)),
         pltpu.SemaphoreType.DMA((13,)),
         pltpu.SemaphoreType.DMA((16,)),
     ]

time: 93.1 us -> 91.1 us (0.979)
  Pallas kernels: 91.6 us -> 89.7 us
    pallas_call x1, Pallas kernels: 88.2 us -> 86.3 us  [body(): pl.pallas_call(kernel, out_shape=jax.ShapeDtypeStruct((2, 8, 240, 128), B...]
where the time goes in v5:
time: 91.1 us; the launch traced here: 90.9 us
  Pallas kernels  89.7 us (98%)
  between operations  1.28 us (1%)
    pallas_call x1, Pallas kernels, body(): pl.pallas_call(kernel, out_shape=jax.ShapeDtypeStruct((2, 8, 240, 128), B...  86.3 us
    pallas_call x1, Pallas kernels, body(): pl.pallas_call(lay_kernel, out_shape=(jax.ShapeDtypeStruct((12, 48, N), F...  3.4 us

profile of v5, /device:TPU:1, one launch (start us, length us, event | category | flops | bytes accessed | tf_op | source)
XLA Modules:
  0.0 90.9 jit_solution(8293026529511482916)
XLA Ops:
  1.3 86.3 %shard_map.149.r6 = bf16[2,8,240,128]{3,2,1,0:T(8,128)(2,1)} custom-call(f32[1]{0:T(128)S(6)} %copy.16.occ, bf16[128,384]{1,0:T(8,128)(2,1)} %bitcast.5, s32[2,512]{1,0:T(2,128)} %rest_1_.1, f32[12,48,192]{2,1,0:T(8,128)} %bitcast.4, bf16[2,512,384]{2,1,0:T(8,128)(2,1)} %constant.20.clone.rest_3_, bf16[2,256,512]{2,1,0:T(8,128)(2,1)} %constant.21.clone.rest_4_, ...), custom_call_target="tpu_custom_call" | custom-call | tf_op jit(solution)/shard_map/pallas_call | solution.py:595
  87.5 3.4 %shard_map.150 = (f32[12,48,192]{2,1,0:T(8,128)}, f32[3,12,48,192]{3,2,1,0:T(8,128)}) custom-call(bf16[2,8,240,128]{3,2,1,0:T(8,128)(2,1)} %shard_map.149.r6), custom_call_target="tpu_custom_call" | custom-call | tf_op jit(solution)/shard_map/pallas_call | solution.py:603

commit v6 on v5

--- a/solution.py
+++ b/solution.py
@@ -261,7 +261,7 @@
     out, near, rest = rest[0], rest[1:14], rest[14:]
     orb, sticks, core, ta, tyc, ry, rx, rz, gz, ryi, rxi, qx, qy = near
     (
-    ty, tx, s1, r1a, r1b, core_out, core_in, planes, part, r2a, sums, r2b, s3, r3a, r3b, s4, r4c,
+    ty, tx, s1, r1a, r1b, core_out, core_in, planes, part, r2a, sums, r2b, s3, r3b, s4, r4c,
     s5, r5b, wide, r6, send, recv, load, store,
     ) = rest
     band, px, py = lax.axis_index("band"), lax.axis_index("px"), lax.axis_index("py")
@@ -331,9 +331,14 @@
     pl.semaphore_wait(bar, 22 + jnp.where(band != px, 1, 0))
 
     phase("e1_y")
-    flights = [copy(s1.at[ring(cy, d, 8)], r1a.at[cy], at(y=ring(cy, d, 8))) for d in FAR_FIRST]
+    x_own = 4 * (cx // 4)
+    x_far = 4 - x_own
+    firsts = []
+    for start in (x_far, x_own):
+        cut = pl.ds(start, 4)
+        firsts.append([copy(s1.at[ring(cy, d, 8), cut], r1a.at[cy, cut], at(y=ring(cy, d, 8))) for d in FAR_FIRST])
     core_copy = pltpu.make_async_remote_copy(
-        src_ref=core_out, dst_ref=core_in, send_sem=send.at[179], recv_sem=recv.at[179],
+        src_ref=core_out, dst_ref=core_in, send_sem=send.at[239], recv_sem=recv.at[239],
         device_id=swapped, device_id_type=MESH,
     )
 
@@ -349,14 +354,17 @@
     for k in (4, 5, 6):
         loads[k].wait()
     stage_tables(tyc, ty, tx)
-    for f in flights:
-        f.wait()
-    phase("e1_x_core")
     arrival = count[0] - 1
-    flights = [
-        copy(r1a.at[:, ring(cx, d, 8)], r1b.at[:, cx], at(x=ring(cx, d, 8)), arrival + d) for d in FAR_FIRST
-    ]
     count[0] += 7
+    flights = []
+    for h, start in enumerate((x_far, x_own)):
+        for f in firsts[h]:
+            f.wait()
+        phase("e1_x_core" if h else "e1_x_far")
+        for m in (2, 1, 3, 0)[: 4 - h]:
+            x = start + lax.rem(cx + m, 4)
+            d = lax.rem(x + 8 - cx, 8)
+            flights.append(copy(r1a.at[:, x], r1b.at[:, cx], at(x=x), arrival + d))
     for y in range(8):
         r1b[y, cx] = r1a[y, cx]
 
@@ -425,19 +433,16 @@
 
     phase("pack")
     s3[...] = stage_pack(acc).reshape(8, 8, 128)
-    phase("e3_y")
-    flights = [copy(s3.at[ring(cy, d, 8)], r3a.at[cy], at(y=ring(cy, d, 8))) for d in FAR_FIRST]
-    r3a[cy] = s3[cy]
+    phase("e3")
+    flights = []
+    for e in FAR_FIRST + (0,):
+        for d in FAR_FIRST + (0,):
+            if e or d:
+                y, x = ring(cy, e, 8), ring(cx, d, 8)
+                flights.append(copy(s3.at[y, pl.ds(x, 1)], r3b.at[cy, pl.ds(cx, 1)], at(x=x, y=y)))
+    r3b[cy, pl.ds(cx, 1)] = s3[cy, pl.ds(cx, 1)]
     for f in flights:
         f.wait()
-    phase("e3_x")
-    flights = [
-        copy(r3a.at[:, pl.ds(ring(cx, d, 8), 1)], r3b.at[:, pl.ds(cx, 1)], at(x=ring(cx, d, 8))) for d in FAR_FIRST
-    ]
-    r3b[:, pl.ds(cx, 1)] = r3a[:, pl.ds(cx, 1)]
-    for f in flights:
-        f.wait()
-    phase("z")
     for k in (7, 8, 9, 10, 11, 12):
         loads[k].wait()
     turned = stage_z(r3b[...].reshape(64, 128), qx[py * 16 + px], qy[band], rz, gz)
@@ -580,15 +585,14 @@
         pltpu.VMEM((8, 3, 16, 256), BF),
         pltpu.VMEM((8, 8, 128), F32),
         pltpu.VMEM((8, 8, 128), F32),
-        pltpu.VMEM((8, 8, 128), F32),
         pltpu.VMEM((4, 3, 16, 128), F32),
         pltpu.VMEM((2, 4, 3, 8, 128), F32),
         pltpu.VMEM((2, 8, 16, 128), BF),
         pltpu.VMEM((2, 8, 16, 128), BF),
         pltpu.VMEM((256, 128), F32),
         pltpu.VMEM((2, 8, 240, 128), BF),
-        pltpu.SemaphoreType.DMA((180,)),
-        pltpu.SemaphoreType.DMA((180,)),
+        pltpu.SemaphoreType.DMA((240,)),
+        pltpu.SemaphoreType.DMA((240,)),
         pltpu.SemaphoreType.DMA((13,)),
         pltpu.SemaphoreType.DMA((16,)),
     ]

time: 91.1 us -> 89.3 us (0.980)
  Pallas kernels: 89.7 us -> 87.9 us
    pallas_call x1, Pallas kernels: 86.3 us -> 84.5 us  [body(): pl.pallas_call(kernel, out_shape=jax.ShapeDtypeStruct((2, 8, 240, 128), B...]
where the time goes in v6:
time: 89.3 us; the launch traced here: 89.2 us
  Pallas kernels  87.9 us (98%)
  between operations  1.28 us (1%)
    pallas_call x1, Pallas kernels, body(): pl.pallas_call(kernel, out_shape=jax.ShapeDtypeStruct((2, 8, 240, 128), B...  84.5 us
    pallas_call x1, Pallas kernels, body(): pl.pallas_call(lay_kernel, out_shape=(jax.ShapeDtypeStruct((12, 48, N), F...  3.4 us

profile of v6, /device:TPU:1, one launch (start us, length us, event | category | flops | bytes accessed | tf_op | source)
XLA Modules:
  0.0 89.2 jit_solution(14706351642966755509)
XLA Ops:
  1.3 84.5 %shard_map.149.r6 = bf16[2,8,240,128]{3,2,1,0:T(8,128)(2,1)} custom-call(f32[1]{0:T(128)S(6)} %copy.16.occ, bf16[128,384]{1,0:T(8,128)(2,1)} %bitcast.5, s32[2,512]{1,0:T(2,128)} %rest_1_.1, f32[12,48,192]{2,1,0:T(8,128)} %bitcast.4, bf16[2,512,384]{2,1,0:T(8,128)(2,1)} %constant.20.clone.rest_3_, bf16[2,256,512]{2,1,0:T(8,128)(2,1)} %constant.21.clone.rest_4_, ...), custom_call_target="tpu_custom_call" | custom-call | tf_op jit(solution)/shard_map/pallas_call | solution.py:599
  85.8 3.4 %shard_map.150 = (f32[12,48,192]{2,1,0:T(8,128)}, f32[3,12,48,192]{3,2,1,0:T(8,128)}) custom-call(bf16[2,8,240,128]{3,2,1,0:T(8,128)(2,1)} %shard_map.149.r6), custom_call_target="tpu_custom_call" | custom-call | tf_op jit(solution)/shard_map/pallas_call | solution.py:607

commit v7 on v5

--- a/solution.py
+++ b/solution.py
@@ -303,8 +303,9 @@
         hail(swapped)
 
     loads = {}
-    for k in (0, 1, 3, 2, 4, 5, 6, 7, 8, 9, 10, 11, 12):
+    for k in range(13):
         loads[k] = pltpu.make_async_copy(far[k], near[k], load.at[k])
+    for k in (0, 3, 1, 2):
         loads[k].start()
     count = [0]
 
@@ -324,6 +325,8 @@
         loads[k].wait()
     mine = pl.ds(pl.multiple_of(py * 128, 128), 128)
     s1[...] = stage_columns(orb[...], sticks[0:1, mine], sticks[1:2, mine], px, ta).reshape(8, 8, 8, 128)
+    for k in range(4, 13):
+        loads[k].start()
     loads[2].wait()
     for j in range(3):
         core_out[j] = core[:, pl.ds(3 * band + j, 1)].reshape(12, N)
@@ -331,7 +334,12 @@
     pl.semaphore_wait(bar, 22 + jnp.where(band != px, 1, 0))
 
     phase("e1_y")
-    flights = [copy(s1.at[ring(cy, d, 8)], r1a.at[cy], at(y=ring(cy, d, 8))) for d in FAR_FIRST]
+    x_own = 4 * (cx // 4)
+    x_far = 4 - x_own
+    firsts = []
+    for start in (x_far, x_own):
+        cut = pl.ds(start, 4)
+        firsts.append([copy(s1.at[ring(cy, d, 8), cut], r1a.at[cy, cut], at(y=ring(cy, d, 8))) for d in FAR_FIRST])
     core_copy = pltpu.make_async_remote_copy(
         src_ref=core_out, dst_ref=core_in, send_sem=send.at[179], recv_sem=recv.at[179],
         device_id=swapped, device_id_type=MESH,
@@ -349,14 +357,17 @@
     for k in (4, 5, 6):
         loads[k].wait()
     stage_tables(tyc, ty, tx)
-    for f in flights:
-        f.wait()
-    phase("e1_x_core")
     arrival = count[0] - 1
-    flights = [
-        copy(r1a.at[:, ring(cx, d, 8)], r1b.at[:, cx], at(x=ring(cx, d, 8)), arrival + d) for d in FAR_FIRST
-    ]
     count[0] += 7
+    flights = []
+    for h, start in enumerate((x_far, x_own)):
+        for f in firsts[h]:
+            f.wait()
+        phase("e1_x_core" if h else "e1_x_far")
+        for m in (2, 1, 3, 0)[: 4 - h]:
+            x = start + lax.rem(cx + m, 4)
+            d = lax.rem(x + 8 - cx, 8)
+            flights.append(copy(r1a.at[:, x], r1b.at[:, cx], at(x=x), arrival + d))
     for y in range(8):
         r1b[y, cx] = r1a[y, cx]
 
@@ -476,24 +487,22 @@
     rho, hart, gx, gy, gzz = stage_x(a[:12], g, rxi)
     value = stage_potential(rho, hart, gx, gy, gzz)
 
-    r6[cc, cz] = stage_block([value, gx, gy, gzz])
+    r6[cz] = stage_block([value, gx, gy, gzz])
     phase("e6")
     chunks = (pl.ds(0, 128), pl.ds(128, 112))
     hops, relays, last, home = {}, {}, [], []
 
     def block(away):
-        return r6.at[cc, ring(cz, away % 8, 8)]
+        return r6.at[ring(cz, away % 8, 8)]
 
     def go(ref, away):
         return copy(ref, ref, at(z=ring(cz, away % 8, 8)))
 
     def settle(away):
-        last.append(copy(block(away), block(away), at(c=other)))
-        for c in (cc, other):
-            k = len(home)
-            ref = (c, ring(cz, away % 8, 8))
-            home.append(pltpu.make_async_copy(r6.at[ref], out.at[ref], store.at[k]))
-        home[-2].start()
+        slot = out.at[cc, ring(cz, away % 8, 8)]
+        last.append(copy(block(away), slot, at(c=other)))
+        home.append(pltpu.make_async_copy(block(away), slot, store.at[len(home)]))
+        home[-1].start()
 
     for d in (2, -2):
         for h in (0, 1):
@@ -520,12 +529,9 @@
     relays[4, 0].wait_recv()
     relays[-4, 1].wait_recv()
     settle(4)
-    for k in range(8):
-        last[k].wait()
-        home[2 * k + 1].start()
     for f in list(hops.values()) + list(relays.values()):
         f.wait_send()
-    for f in home:
+    for f in last + home:
         f.wait()
     phase(None)
 
@@ -586,7 +592,7 @@
         pltpu.VMEM((2, 8, 16, 128), BF),
         pltpu.VMEM((2, 8, 16, 128), BF),
         pltpu.VMEM((256, 128), F32),
-        pltpu.VMEM((2, 8, 240, 128), BF),
+        pltpu.VMEM((8, 240, 128), BF),
         pltpu.SemaphoreType.DMA((180,)),
         pltpu.SemaphoreType.DMA((180,)),
         pltpu.SemaphoreType.DMA((13,)),

time: 91.1 us -> 89.9 us (0.987)
  Pallas kernels: 89.7 us -> 88.4 us
    pallas_call x1, Pallas kernels: 86.3 us -> 85 us  [body(): pl.pallas_call(kernel, out_shape=jax.ShapeDtypeStruct((2, 8, 240, 128), B...]
where the time goes in v7:
time: 89.9 us; the launch traced here: 89.7 us
  Pallas kernels  88.4 us (98%)
  between operations  1.28 us (1%)
    pallas_call x1, Pallas kernels, body(): pl.pallas_call(kernel, out_shape=jax.ShapeDtypeStruct((2, 8, 240, 128), B...  85 us
    pallas_call x1, Pallas kernels, body(): pl.pallas_call(lay_kernel, out_shape=(jax.ShapeDtypeStruct((12, 48, N), F...  3.4 us

profile of v7, /device:TPU:1, one launch (start us, length us, event | category | flops | bytes accessed | tf_op | source)
XLA Modules:
  0.0 89.7 jit_solution(14583833600821319679)
XLA Ops:
  1.3 85.0 %shard_map.149.r6 = bf16[2,8,240,128]{3,2,1,0:T(8,128)(2,1)} custom-call(f32[1]{0:T(128)S(6)} %copy.16.occ, bf16[128,384]{1,0:T(8,128)(2,1)} %bitcast.5, s32[2,512]{1,0:T(2,128)} %rest_1_.1, f32[12,48,192]{2,1,0:T(8,128)} %bitcast.4, bf16[2,512,384]{2,1,0:T(8,128)(2,1)} %constant.20.clone.rest_3_, bf16[2,256,512]{2,1,0:T(8,128)(2,1)} %constant.21.clone.rest_4_, ...), custom_call_target="tpu_custom_call" | custom-call | tf_op jit(solution)/shard_map/pallas_call | solution.py:601
  86.3 3.4 %shard_map.150 = (f32[12,48,192]{2,1,0:T(8,128)}, f32[3,12,48,192]{3,2,1,0:T(8,128)}) custom-call(bf16[2,8,240,128]{3,2,1,0:T(8,128)(2,1)} %shard_map.149.r6), custom_call_target="tpu_custom_call" | custom-call | tf_op jit(solution)/shard_map/pallas_call | solution.py:609
